TPU v7x, 128 devices: a whole 4x4x4 slice. The times are simulated.
128 devices in a mesh: layer: 2 (over core), px: 16 (over x, z), py: 4 (over y).
Axes of the slice: x: 4, y: 4, z: 4, core: 2. Of those that a mesh axis runs over, the one named last changes fastest.
Arguments:
- right_side: float32 [8, 2048, 4096], P('layer', 'px', 'py'), may hold values from -30 to 30
- row_conduct: float32 [8, 2048, 4096], P('layer', 'px', 'py'), may hold values from 0.5 to 2
- column_conduct: float32 [8, 2048, 4096], P('layer', 'px', 'py'), may hold values from 0.5 to 2
- via_conduct: float32 [8, 2048, 4096], P('layer', 'px', 'py'), may hold values from 0.5 to 4
- via_mask: int32 [8, 2048, 4096], P('layer', 'px', 'py'), may hold values 0 or 1
- ground_conduct: float32 [8, 2048, 4096], P('layer', 'px', 'py'), may hold values from 0.01 to 0.1
Outputs:
- solution_field: float32 [8, 2048, 4096], P('layer', 'px', 'py')
- residual: float32 [8, 2048, 4096], P('layer', 'px', 'py')
All inputs are finite; a program needn't handle non-finite values. No bound on the sum of `via_mask` on one device may be relied on, other than what follows from the above.
Results may differ from a plain program's by a relative error of at most 0.0001.
Values sent between devices are 32-bit elements; how exact they have to be, the bound alone decides.
A program may use at most 128 MiB of HBM per device.

v0:
```python
import jax
import jax.numpy as jnp
from jax import lax
from jax.sharding import Mesh
from jax.sharding import PartitionSpec as P

ITERS = 2
LAYER_PX_PY = ("layer", "px_0", "px_1", "py")
PX = ("px_0", "px_1")


def extended(value, sides, width):
    edges = {}
    for axis, dim in sides:
        count, length = (lax.axis_size(axis), value.shape[dim])
        up = [(i, (i + 1) % count) for i in range(count - 1)]
        last = lax.slice_in_dim(value, length - width, length, axis=dim)
        initial = lax.slice_in_dim(value, 0, width, axis=dim)
        edges[dim] = (
            lax.ppermute(last, axis, up),
            lax.ppermute(initial, axis, [(b, a) for a, b in up]),
        )
    done = []
    for _, dim in sides:
        low, high = edges[dim]
        around = [(width, width) if d in done else (0, 0) for d in range(value.ndim)]
        value = jnp.concatenate([jnp.pad(low, around), value, jnp.pad(high, around)], axis=dim)
        done.append(dim)
    return value


def by_axis(value, axes):
    for axis in axes:
        value = lax.psum(value, axis)
    return value


def from_behind(value, axis, by):
    count = lax.axis_size(axis)
    pairs = [(i, i + by) for i in range(count) if 0 <= i + by < count]
    return lax.ppermute(value, axis, pairs)


def factor_layers(diagonal, vertical, vertical_below, carried):
    gains = []
    inverses = []
    previous = carried
    for index in range(diagonal.shape[0]):
        inverse = 1.0 / (diagonal[index] - vertical_below[index] * previous)
        previous = vertical[index] * inverse
        gains.append(previous)
        inverses.append(inverse)
    return (jnp.stack(gains), jnp.stack(inverses))


def forward_layers(residual, vertical_below, inverses, carried):
    values = []
    previous = carried
    for index in range(residual.shape[0]):
        previous = (residual[index] + vertical_below[index] * previous) * inverses[index]
        values.append(previous)
    return jnp.stack(values)


def back_layers(forward, gains, carried):
    count = forward.shape[0]
    values = [None] * count
    following = carried
    for index in range(count - 1, -1, -1):
        following = forward[index] + gains[index] * following
        values[index] = following
    return jnp.stack(values)


def operate(field, coeffs):
    diagonal, row_conduct, row_upper, column_conduct, column_left, vertical, vertical_below = coeffs
    padded = extended(field, (("layer", 0), (PX, 1), ("py", 2)), 1)
    return (
        diagonal * field
        - row_conduct * padded[1:-1, 2:, 1:-1]
        - row_upper * padded[1:-1, :-2, 1:-1]
        - column_conduct * padded[1:-1, 1:-1, 2:]
        - column_left * padded[1:-1, 1:-1, :-2]
        - vertical * padded[2:, 1:-1, 1:-1]
        - vertical_below * padded[:-2, 1:-1, 1:-1]
    )


def paired_sums(residual, precond, image):
    return (
        by_axis(jnp.sum(residual * precond), LAYER_PX_PY),
        by_axis(jnp.sum(image * precond), LAYER_PX_PY),
    )


def shards(right_side, row_conduct, column_conduct, via_conduct, via_mask, ground_conduct):
    depth = right_side.shape[0]
    members = lax.axis_size("layer")
    layers_total = depth * members
    level = lax.axis_index("layer") * depth + jnp.arange(depth, dtype=jnp.int32)
    keep = (level < layers_total - 1).astype(jnp.float32)[:, None, None]
    vertical = via_conduct * via_mask.astype(jnp.float32) * keep
    row_edge = from_behind(row_conduct[:, -1:, :], PX, 1)
    row_upper = jnp.concatenate([row_edge, row_conduct[:, :-1, :]], axis=1)
    column_edge = from_behind(column_conduct[:, :, -1:], "py", 1)
    column_left = jnp.concatenate([column_edge, column_conduct[:, :, :-1]], axis=2)
    vertical_edge = from_behind(vertical[-1:], "layer", 1)
    vertical_below = jnp.concatenate([vertical_edge, vertical[:-1]], axis=0)
    diagonal = (
        ground_conduct
        + row_conduct
        + row_upper
        + column_conduct
        + column_left
        + vertical
        + vertical_below
    )
    coeffs = (
        diagonal,
        row_conduct,
        row_upper,
        column_conduct,
        column_left,
        vertical,
        vertical_below,
    )
    plane = jnp.zeros_like(right_side[0])
    carried = plane
    gains, inverses = factor_layers(diagonal, vertical, vertical_below, carried)
    carried = from_behind(gains[-1], "layer", 1)
    gains, inverses = factor_layers(diagonal, vertical, vertical_below, carried)

    def precondition(residual):
        incoming = plane
        forward = forward_layers(residual, vertical_below, inverses, incoming)
        incoming = from_behind(forward[-1], "layer", 1)
        forward = forward_layers(residual, vertical_below, inverses, incoming)
        returning = plane
        solved = back_layers(forward, gains, returning)
        returning = from_behind(solved[0], "layer", -1)
        return back_layers(forward, gains, returning)

    solution_field = jnp.zeros_like(right_side)
    residual = right_side
    precond = precondition(residual)
    image = operate(precond, coeffs)
    rho, curvature = paired_sums(residual, precond, image)
    alpha = rho / curvature
    direction, along = (precond, image)
    for step in range(ITERS):
        solution_field = solution_field + alpha * direction
        residual = residual - alpha * along
        if step + 1 < ITERS:
            precond = precondition(residual)
            image = operate(precond, coeffs)
            rho_next, curvature = paired_sums(residual, precond, image)
            ratio = rho_next / rho
            alpha = rho_next / (curvature - ratio * rho_next / alpha)
            direction = precond + ratio * direction
            along = image + ratio * along
            rho = rho_next
    return (solution_field, residual)


def solution(mesh):
    split = Mesh(
        mesh.devices.reshape(mesh.shape["layer"], 4, 4, mesh.shape["py"]),
        ("layer", "px_0", "px_1", "py"),
    )
    return jax.shard_map(
        shards,
        mesh=split,
        in_specs=(
            P("layer", PX, "py"),
            P("layer", PX, "py"),
            P("layer", PX, "py"),
            P("layer", PX, "py"),
            P("layer", PX, "py"),
            P("layer", PX, "py"),
        ),
        out_specs=(P("layer", PX, "py"), P("layer", PX, "py")),
        check_vma=False,
    )
```

profile of v0, /device:TPU:2, one launch (start us, length us, event | category | flops | bytes accessed | tf_op | source)
XLA Modules:
  0.0 200.5 jit_solution(8595721129554607159)
XLA Ops:
  0.7 2.9 %multiply_multiply_fusion = f32[4,128,1024]{2,1,0:T(8,128)S(1)} fusion(f32[4,128,1024]{2,1,0:T(8,128)} %param.9, s32[4,128,1024]{2,1,0:T(8,128)} %param.10, f32[4]{0:T(128)S(1)} %compare_convert_fusion), kind=kLoop, calls=%fused_computation.59 | loop fusion | flops 1572864 | bytes 6291472 | tf_op jit(solution)/shard_map/mul | solution.py:102
  3.7 1.9 collective-permute-start
  5.6 3.8 %collective-permute-start.1 = (f32[4,1,1024]{2,1,0:T(1,128)S(1)}, f32[4,1,1024]{2,1,0:T(1,128)S(1)}, u32[]{:S(2)}, u32[]{:S(2)}) collective-permute-start(f32[4,1,1024]{2,1,0:T(1,128)S(1)} %slice.173), channel_id=1, source_target_pairs={{0,4},{4,8},{8,12},{12,16},{16,20},{20,24},{24,28},{28,32},{32,36}... | collective-permute-start | bytes 49160 | tf_op jit(solution)/shard_map/ppermute | solution.py:41
  9.6 3.5 %collective-permute-start.2 = (f32[4,128,1]{2,1,0:T(8,128)S(1)}, f32[4,128,1]{2,1,0:T(8,128)S(1)}, u32[]{:S(2)}, u32[]{:S(2)}) collective-permute-start(f32[4,128,1]{2,1,0:T(8,128)S(1)} %slice.175), channel_id=1, source_target_pairs={{0,1},{1,2},{2,3},{4,5},{5,6},{6,7},{8,9},{9,10},{10,11},{12,13},{... | collective-permute-start | bytes 6152 | tf_op jit(solution)/shard_map/ppermute | solution.py:41
  13.2 4.7 %collective-permute-done.2 = f32[4,128,1]{2,1,0:T(8,128)S(1)} collective-permute-done((f32[4,128,1]{2,1,0:T(8,128)S(1)}, f32[4,128,1]{2,1,0:T(8,128)S(1)}, u32[]{:S(2)}, u32[]{:S(2)}) %collective-permute-start.2) | collective-permute-done | bytes 2080 | tf_op jit(solution)/shard_map/ppermute | solution.py:41
  17.9 1.8 add_add_fusion
  19.8 0.4 fusion.30
  20.2 1.5 collective-permute-start.3
  21.6 1.5 collective-permute-done.3
  23.1 0.9 fusion.37
  24.1 2.3 %collective-permute-start.4 = (f32[128,1024]{1,0:T(8,128)S(1)}, f32[128,1024]{1,0:T(8,128)S(1)}, u32[]{:S(2)}, u32[]{:S(2)}) collective-permute-start(f32[128,1024]{1,0:T(8,128)S(1)} %get-tuple-element.40), channel_id=1, source_target_pairs={{0,64},{1,65},{2,66},{3,67},{4,68},{5,69},{6,70},{7,71},{8,72},{9,... | collective-permute-start | bytes 1572872 | tf_op jit(solution)/shard_map/ppermute | solution.py:41
  26.4 1.5 collective-permute-done.4
  27.9 1.0 multiply_add_fusion.8
  28.9 1.3 collective-permute-start.5
  30.2 2.5 %collective-permute-done.5 = f32[128,1024]{1,0:T(8,128)S(1)} collective-permute-done((f32[128,1024]{1,0:T(8,128)S(1)}, f32[128,1024]{1,0:T(8,128)S(1)}, u32[]{:S(2)}, u32[]{:S(2)}) %collective-permute-start.5) | collective-permute-done | bytes 524320 | tf_op jit(solution)/shard_map/ppermute | solution.py:41
  32.7 0.3 multiply_add_fusion.7
  33.0 2.1 %collective-permute-start.6 = (f32[1,128,1024]{2,1,0:T(8,128)S(1)}, f32[1,128,1024]{2,1,0:T(8,128)S(1)}, u32[]{:S(2)}, u32[]{:S(2)}) collective-permute-start(f32[1,128,1024]{2,1,0:T(8,128)S(1)} %bitcast.233), channel_id=1, source_target_pairs={{0,64},{1,65},{2,66},{3,67},{4,68},{5,69},{6,70},{7,71},{8,72},{9,... | collective-permute-start | bytes 1572872 | tf_op jit(solution)/shard_map/ppermute | solution.py:20
  35.1 1.5 collective-permute-done.6
  36.7 0.4 constant_dynamic-update-slice_fusion.4
  37.1 0.3 copy-done.31
  37.4 1.3 collective-permute-start.7
  38.8 0.2 pad_maximum_fusion.15
  39.1 4.0 %collective-permute-start.9 = (f32[4,1,1024]{2,1,0:T(1,128)S(1)}, f32[4,1,1024]{2,1,0:T(1,128)S(1)}, u32[]{:S(2)}, u32[]{:S(2)}) collective-permute-start(f32[4,1,1024]{2,1,0:T(1,128)S(1)} %get-tuple-element.54), channel_id=1, source_target_pairs={{0,4},{4,8},{8,12},{12,16},{16,20},{20,24},{24,28},{28,32},{32,36}... | collective-permute-start | bytes 49160 | tf_op jit(solution)/shard_map/ppermute | solution.py:20
  43.0 4.1 %collective-permute-start.8 = (f32[4,1,1024]{2,1,0:T(1,128)S(1)}, f32[4,1,1024]{2,1,0:T(1,128)S(1)}, u32[]{:S(2)}, u32[]{:S(2)}) collective-permute-start(f32[4,1,1024]{2,1,0:T(1,128)S(1)} %get-tuple-element.55), channel_id=1, source_target_pairs={{4,0},{8,4},{12,8},{16,12},{20,16},{24,20},{28,24},{32,28},{36,32}... | collective-permute-start | bytes 49160 | tf_op jit(solution)/shard_map/ppermute | solution.py:21
  47.3 1.3 collective-permute-start.10
  48.6 5.0 %collective-permute-start.11 = (f32[4,128,1]{2,1,0:T(8,128)S(1)}, f32[4,128,1]{2,1,0:T(8,128)S(1)}, u32[]{:S(2)}, u32[]{:S(2)}) collective-permute-start(f32[4,128,1]{2,1,0:T(8,128)S(1)} %get-tuple-element.53), channel_id=1, source_target_pairs={{0,1},{1,2},{2,3},{4,5},{5,6},{6,7},{8,9},{9,10},{10,11},{12,13},{... | collective-permute-start | bytes 6152 | tf_op jit(solution)/shard_map/ppermute | solution.py:20
  53.8 0.7 copy-done.33
  54.6 4.2 %collective-permute-done.10 = f32[4,128,1]{2,1,0:T(8,128)S(1)} collective-permute-done((f32[4,128,1]{2,1,0:T(8,128)S(1)}, f32[4,128,1]{2,1,0:T(8,128)S(1)}, u32[]{:S(2)}, u32[]{:S(2)}) %collective-permute-start.10) | collective-permute-done | bytes 2080 | tf_op jit(solution)/shard_map/ppermute | solution.py:21
  58.8 1.2 collective-permute-done.11
  60.0 9.9 %multiply_reduce_fusion.2 = (f32[]{:T(128)}, f32[]{:T(128)}, f32[4,128,1024]{2,1,0:T(8,128)}) fusion(f32[1,128,1024]{2,1,0:T(8,128)S(1)} %bitcast.235, f32[1,128,1024]{2,1,0:T(8,128)S(1)} %bitcast.245, f32[1,128,1024]{2,1,0:T(8,128)S(1)} %bitcast.242, f32[1,128,1024]{2,1,0:T(8,128)S(1)} %get-tuple-element.33, f32[4,128,1024]{2,1,0:T(8,128)S(1)} %copy-done.5, ...), kind=kLoop, calls=%fused_computation.56 | loop fusion | flops 25690112 | bytes 25219080 | tf_op jit(solution)/shard_map/reduce_sum | solution.py:92
  69.9 3.1 %all-reduce.15 = (f32[]{:T(128)}, f32[]{:T(128)}) all-reduce(f32[]{:T(128)} %get-tuple-element.5, f32[]{:T(128)} %get-tuple-element.4), channel_id=1, replica_groups=mesh['layer'=2,'px_0'=4,'px_1'=4,'py'=4] {'layer'}, use_global_device_ids=true, to_apply=%region_1.2 | all-reduce | flops 2 | bytes 16 | tf_op jit(solution)/shard_map/psum | solution.py:34
  73.0 9.3 %all-reduce.13 = (f32[]{:T(128)}, f32[]{:T(128)}) all-reduce(f32[]{:T(128)} %get-tuple-element.20, f32[]{:T(128)} %get-tuple-element.21), channel_id=1, replica_groups=mesh['layer'=2,'px_0'=4,'px_1'=4,'py'=4] {'px_0'}, use_global_device_ids=true, to_apply=%region_2.3 | all-reduce | flops 2 | bytes 16 | tf_op jit(solution)/shard_map/psum | solution.py:34
  82.3 8.7 %all-reduce.11 = (f32[]{:T(128)}, f32[]{:T(128)}) all-reduce(f32[]{:T(128)} %get-tuple-element.16, f32[]{:T(128)} %get-tuple-element.17), channel_id=1, replica_groups=mesh['layer'=2,'px_0'=4,'px_1'=4,'py'=4] {'px_1'}, use_global_device_ids=true, to_apply=%region_3.4 | all-reduce | flops 2 | bytes 16 | tf_op jit(solution)/shard_map/psum | solution.py:34
  91.0 12.8 %all-reduce.9 = (f32[]{:T(128)}, f32[]{:T(128)}) all-reduce(f32[]{:T(128)} %get-tuple-element.12, f32[]{:T(128)} %get-tuple-element.13), channel_id=1, replica_groups=mesh['layer'=2,'px_0'=4,'px_1'=4,'py'=4] {'py'}, use_global_device_ids=true, to_apply=%region_4.5 | all-reduce | flops 2 | bytes 16 | tf_op jit(solution)/shard_map/psum | solution.py:34
  105.3 2.8 %multiply_subtract_fusion.1 = f32[4,128,1024]{2,1,0:T(8,128)S(1)} fusion(f32[4,128,1024]{2,1,0:T(8,128)} %param.6, f32[4,128,1024]{2,1,0:T(8,128)} %get-tuple-element.31, f32[]{:T(128)S(6)} %div.44), kind=kLoop, calls=%fused_computation.55 | loop fusion | flops 1048576 | bytes 6291460 | tf_op jit(solution)/shard_map/sub | solution.py:152
  108.2 0.7 add_multiply_fusion.3
  108.8 1.6 collective-permute-start.12
  110.5 1.3 collective-permute-done.12
  111.8 1.0 multiply_add_fusion.4
  112.8 1.3 collective-permute-start.13
  114.1 2.5 %collective-permute-done.13 = f32[128,1024]{1,0:T(8,128)S(1)} collective-permute-done((f32[128,1024]{1,0:T(8,128)S(1)}, f32[128,1024]{1,0:T(8,128)S(1)}, u32[]{:S(2)}, u32[]{:S(2)}) %collective-permute-start.13) | collective-permute-done | bytes 524320 | tf_op jit(solution)/shard_map/ppermute | solution.py:41
  116.6 0.3 multiply_add_fusion.3
  116.9 2.1 %collective-permute-start.14 = (f32[1,128,1024]{2,1,0:T(8,128)S(1)}, f32[1,128,1024]{2,1,0:T(8,128)S(1)}, u32[]{:S(2)}, u32[]{:S(2)}) collective-permute-start(f32[1,128,1024]{2,1,0:T(8,128)S(1)} %bitcast.237), channel_id=1, source_target_pairs={{0,64},{1,65},{2,66},{3,67},{4,68},{5,69},{6,70},{7,71},{8,72},{9,... | collective-permute-start | bytes 1572872 | tf_op jit(solution)/shard_map/ppermute | solution.py:20
  119.0 1.5 collective-permute-done.14
  120.5 0.8 constant_dynamic-update-slice_fusion.11
  121.3 1.3 constant_dynamic-update-slice_fusion.10
  122.6 1.3 collective-permute-start.15
  123.9 0.8 constant_dynamic-update-slice_fusion.9
  124.7 0.8 constant_dynamic-update-slice_fusion.8
  125.5 0.2 pad_maximum_fusion.16
  125.8 3.9 %collective-permute-start.17 = (f32[4,1,1024]{2,1,0:T(1,128)S(1)}, f32[4,1,1024]{2,1,0:T(1,128)S(1)}, u32[]{:S(2)}, u32[]{:S(2)}) collective-permute-start(f32[4,1,1024]{2,1,0:T(1,128)S(1)} %get-tuple-element.50), channel_id=1, source_target_pairs={{0,4},{4,8},{8,12},{12,16},{16,20},{20,24},{24,28},{28,32},{32,36}... | collective-permute-start | bytes 49160 | tf_op jit(solution)/shard_map/ppermute | solution.py:20
  129.7 4.3 %collective-permute-start.16 = (f32[4,1,1024]{2,1,0:T(1,128)S(1)}, f32[4,1,1024]{2,1,0:T(1,128)S(1)}, u32[]{:S(2)}, u32[]{:S(2)}) collective-permute-start(f32[4,1,1024]{2,1,0:T(1,128)S(1)} %get-tuple-element.51), channel_id=1, source_target_pairs={{4,0},{8,4},{12,8},{16,12},{20,16},{24,20},{28,24},{32,28},{36,32}... | collective-permute-start | bytes 49160 | tf_op jit(solution)/shard_map/ppermute | solution.py:21
  134.1 0.8 constant_dynamic-update-slice_fusion.7
  135.1 1.3 collective-permute-start.18
  136.4 4.6 %collective-permute-start.19 = (f32[4,128,1]{2,1,0:T(8,128)S(1)}, f32[4,128,1]{2,1,0:T(8,128)S(1)}, u32[]{:S(2)}, u32[]{:S(2)}) collective-permute-start(f32[4,128,1]{2,1,0:T(8,128)S(1)} %get-tuple-element.49), channel_id=1, source_target_pairs={{0,1},{1,2},{2,3},{4,5},{5,6},{6,7},{8,9},{9,10},{10,11},{12,13},{... | collective-permute-start | bytes 6152 | tf_op jit(solution)/shard_map/ppermute | solution.py:20
  141.0 0.8 constant_dynamic-update-slice_fusion.6
  141.8 3.9 %collective-permute-done.18 = f32[4,128,1]{2,1,0:T(8,128)S(1)} collective-permute-done((f32[4,128,1]{2,1,0:T(8,128)S(1)}, f32[4,128,1]{2,1,0:T(8,128)S(1)}, u32[]{:S(2)}, u32[]{:S(2)}) %collective-permute-start.18) | collective-permute-done | bytes 2080 | tf_op jit(solution)/shard_map/ppermute | solution.py:21
  145.8 1.2 collective-permute-done.19
  147.0 10.1 %multiply_reduce_fusion = (f32[]{:T(128)}, f32[]{:T(128)}, f32[4,128,1024]{2,1,0:T(8,128)}) fusion(f32[1,128,1024]{2,1,0:T(8,128)S(1)} %bitcast.239, f32[1,128,1024]{2,1,0:T(8,128)S(1)} %bitcast.251, f32[1,128,1024]{2,1,0:T(8,128)S(1)} %bitcast.248, f32[1,128,1024]{2,1,0:T(8,128)S(1)} %get-tuple-element.24, f32[4,128,1024]{2,1,0:T(8,128)S(1)} %multiply_subtract_fusion.1, ...), kind=kLoop, calls=%fused_computation.53 | loop fusion | flops 25690112 | bytes 25219080 | tf_op jit(solution)/shard_map/reduce_sum | solution.py:92
  157.1 3.1 %all-reduce.14 = (f32[]{:T(128)}, f32[]{:T(128)}) all-reduce(f32[]{:T(128)} %get-tuple-element.3, f32[]{:T(128)} %get-tuple-element.2), channel_id=1, replica_groups=mesh['layer'=2,'px_0'=4,'px_1'=4,'py'=4] {'layer'}, use_global_device_ids=true, to_apply=%region_11.12 | all-reduce | flops 2 | bytes 16 | tf_op jit(solution)/shard_map/psum | solution.py:34
  160.2 9.0 %all-reduce.12 = (f32[]{:T(128)}, f32[]{:T(128)}) all-reduce(f32[]{:T(128)} %get-tuple-element.18, f32[]{:T(128)} %get-tuple-element.19), channel_id=1, replica_groups=mesh['layer'=2,'px_0'=4,'px_1'=4,'py'=4] {'px_0'}, use_global_device_ids=true, to_apply=%region_12.13 | all-reduce | flops 2 | bytes 16 | tf_op jit(solution)/shard_map/psum | solution.py:34
  169.1 9.8 %all-reduce.10 = (f32[]{:T(128)}, f32[]{:T(128)}) all-reduce(f32[]{:T(128)} %get-tuple-element.14, f32[]{:T(128)} %get-tuple-element.15), channel_id=1, replica_groups=mesh['layer'=2,'px_0'=4,'px_1'=4,'py'=4] {'px_1'}, use_global_device_ids=true, to_apply=%region_13.14 | all-reduce | flops 2 | bytes 16 | tf_op jit(solution)/shard_map/psum | solution.py:34
  178.9 10.9 %all-reduce.8 = (f32[]{:T(128)}, f32[]{:T(128)}) all-reduce(f32[]{:T(128)} %get-tuple-element.10, f32[]{:T(128)} %get-tuple-element.11), channel_id=1, replica_groups=mesh['layer'=2,'px_0'=4,'px_1'=4,'py'=4] {'py'}, use_global_device_ids=true, to_apply=%region_14.15 | all-reduce | flops 2 | bytes 16 | tf_op jit(solution)/shard_map/psum | solution.py:34
  194.4 6.0 %multiply_subtract_fusion = (f32[4,128,1024]{2,1,0:T(8,128)}, f32[4,128,1024]{2,1,0:T(8,128)}) fusion(f32[4,128,1024]{2,1,0:T(8,128)} %copy-done.4, f32[4,128,1024]{2,1,0:T(8,128)} %get-tuple-element.22, f32[4,128,1024]{2,1,0:T(8,128)} %get-tuple-element.31, f32[]{:T(128)S(6)} %div.45, f32[]{:T(128)S(6)} %div.47, f32[1,128,1024]{2,1,0:T(8,128)} %bitcast.240, ...), kind=kLoop, calls=%fused_computation.51 | loop fusion | flops 7864320 | bytes 14680076 | tf_op jit(solution)/shard_map/sub | solution.py:152
  (92 shorter events, 1.1 us)
Async XLA Ops:
  0.6 5.0 %copy-start.2 = (f32[4,128,1024]{2,1,0:T(8,128)S(1)}, f32[4,128,1024]{2,1,0:T(8,128)}, u32[]{:S(2)}) copy-start(f32[4,128,1024]{2,1,0:T(8,128)} %param.7) | copy-start | bytes 6291460
  0.7 8.8 %copy-start = (f32[4,128,1024]{2,1,0:T(8,128)S(1)}, f32[4,128,1024]{2,1,0:T(8,128)}, u32[]{:S(2)}) copy-start(f32[4,128,1024]{2,1,0:T(8,128)} %param.8) | copy-start | bytes 6291460
  3.7 14.2 %copy-start.8 = (f32[4,128,1024]{2,1,0:T(8,128)S(1)}, f32[4,128,1024]{2,1,0:T(8,128)}, u32[]{:S(2)}) copy-start(f32[4,128,1024]{2,1,0:T(8,128)} %param.11) | copy-start | bytes 6291460
  3.7 14.2 %collective-permute-start = (f32[1,128,1024]{2,1,0:T(8,128)S(1)}, f32[1,128,1024]{2,1,0:T(8,128)S(1)}, u32[]{:S(2)}, u32[]{:S(2)}) collective-permute-start(f32[1,128,1024]{2,1,0:T(8,128)S(1)} %slice.202), channel_id=1, source_target_pairs={{0,64},{1,65},{2,66},{3,67},{4,68},{5,69},{6,70},{7,71},{8,72},{9,... | collective-permute-start | bytes 1572872 | tf_op jit(solution)/shard_map/ppermute | solution.py:41
  5.6 12.3 %collective-permute-start.1 = (f32[4,1,1024]{2,1,0:T(1,128)S(1)}, f32[4,1,1024]{2,1,0:T(1,128)S(1)}, u32[]{:S(2)}, u32[]{:S(2)}) collective-permute-start(f32[4,1,1024]{2,1,0:T(1,128)S(1)} %slice.173), channel_id=1, source_target_pairs={{0,4},{4,8},{8,12},{12,16},{16,20},{20,24},{24,28},{28,32},{32,36}... | collective-permute-start | bytes 49160 | tf_op jit(solution)/shard_map/ppermute | solution.py:41
  9.6 8.3 %collective-permute-start.2 = (f32[4,128,1]{2,1,0:T(8,128)S(1)}, f32[4,128,1]{2,1,0:T(8,128)S(1)}, u32[]{:S(2)}, u32[]{:S(2)}) collective-permute-start(f32[4,128,1]{2,1,0:T(8,128)S(1)} %slice.175), channel_id=1, source_target_pairs={{0,1},{1,2},{2,3},{4,5},{5,6},{6,7},{8,9},{9,10},{10,11},{12,13},{... | collective-permute-start | bytes 6152 | tf_op jit(solution)/shard_map/ppermute | solution.py:41
  13.2 46.7 %copy-start.6 = (f32[3,128,1024]{2,1,0:T(8,128)}, f32[3,128,1024]{2,1,0:T(8,128)S(1)}, u32[]{:S(2)}) copy-start(f32[3,128,1024]{2,1,0:T(8,128)S(1)} %slice.206) | copy-start | bytes 4718596
  19.7 3.4 %copy-start.5 = (f32[4,128,1024]{2,1,0:T(8,128)S(1)}, f32[4,128,1024]{2,1,0:T(8,128)}, u32[]{:S(2)}) copy-start(f32[4,128,1024]{2,1,0:T(8,128)} %param.6) | copy-start | bytes 6291460
  20.2 2.9 %collective-permute-start.3 = (f32[128,1024]{1,0:T(8,128)S(1)}, f32[128,1024]{1,0:T(8,128)S(1)}, u32[]{:S(2)}, u32[]{:S(2)}) collective-permute-start(f32[128,1024]{1,0:T(8,128)S(1)} %fusion.30), channel_id=1, source_target_pairs={{0,64},{1,65},{2,66},{3,67},{4,68},{5,69},{6,70},{7,71},{8,72},{9,... | collective-permute-start | bytes 1572872 | tf_op jit(solution)/shard_map/ppermute | solution.py:41
  24.0 4.9 %copy-start.25 = (f32[128,1024]{1,0:T(8,128)}, f32[128,1024]{1,0:T(8,128)S(1)}, u32[]{:S(2)}) copy-start(f32[128,1024]{1,0:T(8,128)S(1)} %get-tuple-element.43) | copy-start | bytes 1572868
  24.0 4.9 %copy-start.27 = (f32[128,1024]{1,0:T(8,128)}, f32[128,1024]{1,0:T(8,128)S(1)}, u32[]{:S(2)}) copy-start(f32[128,1024]{1,0:T(8,128)S(1)} %get-tuple-element.45) | copy-start | bytes 1572868
  24.0 4.9 %copy-start.29 = (f32[128,1024]{1,0:T(8,128)}, f32[128,1024]{1,0:T(8,128)S(1)}, u32[]{:S(2)}) copy-start(f32[128,1024]{1,0:T(8,128)S(1)} %get-tuple-element.47) | copy-start | bytes 1572868
  24.0 8.7 %copy-start.11 = (f32[128,1024]{1,0:T(8,128)}, f32[128,1024]{1,0:T(8,128)S(1)}, u32[]{:S(2)}) copy-start(f32[128,1024]{1,0:T(8,128)S(1)} %get-tuple-element.41) | copy-start | bytes 1572868
  24.0 12.6 %copy-start.17 = (f32[128,1024]{1,0:T(8,128)}, f32[128,1024]{1,0:T(8,128)S(1)}, u32[]{:S(2)}) copy-start(f32[128,1024]{1,0:T(8,128)S(1)} %get-tuple-element.42) | copy-start | bytes 1572868
  24.1 12.6 %copy-start.19 = (f32[128,1024]{1,0:T(8,128)}, f32[128,1024]{1,0:T(8,128)S(1)}, u32[]{:S(2)}) copy-start(f32[128,1024]{1,0:T(8,128)S(1)} %get-tuple-element.44) | copy-start | bytes 1572868
  24.1 12.6 %copy-start.21 = (f32[128,1024]{1,0:T(8,128)}, f32[128,1024]{1,0:T(8,128)S(1)}, u32[]{:S(2)}) copy-start(f32[128,1024]{1,0:T(8,128)S(1)} %get-tuple-element.46) | copy-start | bytes 1572868
  24.1 3.8 %collective-permute-start.4 = (f32[128,1024]{1,0:T(8,128)S(1)}, f32[128,1024]{1,0:T(8,128)S(1)}, u32[]{:S(2)}, u32[]{:S(2)}) collective-permute-start(f32[128,1024]{1,0:T(8,128)S(1)} %get-tuple-element.40), channel_id=1, source_target_pairs={{0,64},{1,65},{2,66},{3,67},{4,68},{5,69},{6,70},{7,71},{8,72},{9,... | collective-permute-start | bytes 1572872 | tf_op jit(solution)/shard_map/ppermute | solution.py:41
  28.9 3.8 %collective-permute-start.5 = (f32[128,1024]{1,0:T(8,128)S(1)}, f32[128,1024]{1,0:T(8,128)S(1)}, u32[]{:S(2)}, u32[]{:S(2)}) collective-permute-start(f32[128,1024]{1,0:T(8,128)S(1)} %get-tuple-element.36), channel_id=1, source_target_pairs={{64,0},{65,1},{66,2},{67,3},{68,4},{69,5},{70,6},{71,7},{72,8},{73... | collective-permute-start | bytes 1572872 | tf_op jit(solution)/shard_map/ppermute | solution.py:41
  33.0 3.6 %collective-permute-start.6 = (f32[1,128,1024]{2,1,0:T(8,128)S(1)}, f32[1,128,1024]{2,1,0:T(8,128)S(1)}, u32[]{:S(2)}, u32[]{:S(2)}) collective-permute-start(f32[1,128,1024]{2,1,0:T(8,128)S(1)} %bitcast.233), channel_id=1, source_target_pairs={{0,64},{1,65},{2,66},{3,67},{4,68},{5,69},{6,70},{7,71},{8,72},{9,... | collective-permute-start | bytes 1572872 | tf_op jit(solution)/shard_map/ppermute | solution.py:20
  36.6 0.8 copy-start.31
  37.4 22.6 %copy-start.13 = (f32[128,1024]{1,0:T(8,128)}, f32[128,1024]{1,0:T(8,128)S(1)}, u32[]{:S(2)}) copy-start(f32[128,1024]{1,0:T(8,128)S(1)} %get-tuple-element.34) | copy-start | bytes 1572868
  37.4 22.6 %copy-start.14 = (f32[128,1024]{1,0:T(8,128)}, f32[128,1024]{1,0:T(8,128)S(1)}, u32[]{:S(2)}) copy-start(f32[128,1024]{1,0:T(8,128)S(1)} %get-tuple-element.35) | copy-start | bytes 1572868
  37.4 22.6 %copy-start.23 = (f32[1,128,1024]{2,1,0:T(8,128)}, f32[1,128,1024]{2,1,0:T(8,128)S(1)}, u32[]{:S(2)}) copy-start(f32[1,128,1024]{2,1,0:T(8,128)S(1)} %get-tuple-element.33) | copy-start | bytes 1572868
  37.4 16.4 %collective-permute-start.7 = (f32[1,128,1024]{2,1,0:T(8,128)S(1)}, f32[1,128,1024]{2,1,0:T(8,128)S(1)}, u32[]{:S(2)}, u32[]{:S(2)}) collective-permute-start(f32[1,128,1024]{2,1,0:T(8,128)S(1)} %get-tuple-element.33), channel_id=1, source_target_pairs={{64,0},{65,1},{66,2},{67,3},{68,4},{69,5},{70,6},{71,7},{72,8},{73... | collective-permute-start | bytes 1572872 | tf_op jit(solution)/shard_map/ppermute | solution.py:21
  39.0 21.0 %copy-start.32 = (f32[1,128,1024]{2,1,0:T(8,128)S(1)}, f32[1,128,1024]{2,1,0:T(8,128)}, u32[]{:S(2)}) copy-start(f32[1,128,1024]{2,1,0:T(8,128)} %copy-done.31) | copy-start | bytes 1572868
  39.1 14.6 %collective-permute-start.9 = (f32[4,1,1024]{2,1,0:T(1,128)S(1)}, f32[4,1,1024]{2,1,0:T(1,128)S(1)}, u32[]{:S(2)}, u32[]{:S(2)}) collective-permute-start(f32[4,1,1024]{2,1,0:T(1,128)S(1)} %get-tuple-element.54), channel_id=1, source_target_pairs={{0,4},{4,8},{8,12},{12,16},{16,20},{20,24},{24,28},{28,32},{32,36}... | collective-permute-start | bytes 49160 | tf_op jit(solution)/shard_map/ppermute | solution.py:20
  43.0 10.7 %collective-permute-start.8 = (f32[4,1,1024]{2,1,0:T(1,128)S(1)}, f32[4,1,1024]{2,1,0:T(1,128)S(1)}, u32[]{:S(2)}, u32[]{:S(2)}) collective-permute-start(f32[4,1,1024]{2,1,0:T(1,128)S(1)} %get-tuple-element.55), channel_id=1, source_target_pairs={{4,0},{8,4},{12,8},{16,12},{20,16},{24,20},{28,24},{32,28},{36,32}... | collective-permute-start | bytes 49160 | tf_op jit(solution)/shard_map/ppermute | solution.py:21
  47.3 11.4 %collective-permute-start.10 = (f32[4,128,1]{2,1,0:T(8,128)S(1)}, f32[4,128,1]{2,1,0:T(8,128)S(1)}, u32[]{:S(2)}, u32[]{:S(2)}) collective-permute-start(f32[4,128,1]{2,1,0:T(8,128)S(1)} %get-tuple-element.52), channel_id=1, source_target_pairs={{1,0},{2,1},{3,2},{5,4},{6,5},{7,6},{9,8},{10,9},{11,10},{13,12},{... | collective-permute-start | bytes 6152 | tf_op jit(solution)/shard_map/ppermute | solution.py:21
  48.6 11.3 %collective-permute-start.11 = (f32[4,128,1]{2,1,0:T(8,128)S(1)}, f32[4,128,1]{2,1,0:T(8,128)S(1)}, u32[]{:S(2)}, u32[]{:S(2)}) collective-permute-start(f32[4,128,1]{2,1,0:T(8,128)S(1)} %get-tuple-element.53), channel_id=1, source_target_pairs={{0,1},{1,2},{2,3},{4,5},{5,6},{6,7},{8,9},{9,10},{10,11},{12,13},{... | collective-permute-start | bytes 6152 | tf_op jit(solution)/shard_map/ppermute | solution.py:20
  53.8 0.8 copy-start.33
  105.2 2.8 %copy-start.12 = (f32[128,1024]{1,0:T(8,128)S(1)}, f32[128,1024]{1,0:T(8,128)}, u32[]{:S(2)}) copy-start(f32[128,1024]{1,0:T(8,128)} %copy-done.11) | copy-start | bytes 1572868
  105.3 2.8 %copy-start.26 = (f32[128,1024]{1,0:T(8,128)S(1)}, f32[128,1024]{1,0:T(8,128)}, u32[]{:S(2)}) copy-start(f32[128,1024]{1,0:T(8,128)} %copy-done.25) | copy-start | bytes 1572868
  105.3 2.8 %copy-start.28 = (f32[128,1024]{1,0:T(8,128)S(1)}, f32[128,1024]{1,0:T(8,128)}, u32[]{:S(2)}) copy-start(f32[128,1024]{1,0:T(8,128)} %copy-done.27) | copy-start | bytes 1572868
  105.3 2.8 %copy-start.30 = (f32[128,1024]{1,0:T(8,128)S(1)}, f32[128,1024]{1,0:T(8,128)}, u32[]{:S(2)}) copy-start(f32[128,1024]{1,0:T(8,128)} %copy-done.29) | copy-start | bytes 1572868
  108.1 38.8 %copy-start.4 = (f32[4,128,1024]{2,1,0:T(8,128)}, f32[4,128,1024]{2,1,0:T(8,128)S(1)}, u32[]{:S(2)}) copy-start(f32[4,128,1024]{2,1,0:T(8,128)S(1)} %multiply_subtract_fusion.1) | copy-start | bytes 6291460
  108.1 3.6 %copy-start.18 = (f32[128,1024]{1,0:T(8,128)S(1)}, f32[128,1024]{1,0:T(8,128)}, u32[]{:S(2)}) copy-start(f32[128,1024]{1,0:T(8,128)} %copy-done.17) | copy-start | bytes 1572868
  108.1 3.6 %copy-start.20 = (f32[128,1024]{1,0:T(8,128)S(1)}, f32[128,1024]{1,0:T(8,128)}, u32[]{:S(2)}) copy-start(f32[128,1024]{1,0:T(8,128)} %copy-done.19) | copy-start | bytes 1572868
  108.2 3.6 %copy-start.22 = (f32[128,1024]{1,0:T(8,128)S(1)}, f32[128,1024]{1,0:T(8,128)}, u32[]{:S(2)}) copy-start(f32[128,1024]{1,0:T(8,128)} %copy-done.21) | copy-start | bytes 1572868
  108.8 2.9 %collective-permute-start.12 = (f32[128,1024]{1,0:T(8,128)S(1)}, f32[128,1024]{1,0:T(8,128)S(1)}, u32[]{:S(2)}, u32[]{:S(2)}) collective-permute-start(f32[128,1024]{1,0:T(8,128)S(1)} %add_multiply_fusion.3), channel_id=1, source_target_pairs={{0,64},{1,65},{2,66},{3,67},{4,68},{5,69},{6,70},{7,71},{8,72},{9,... | collective-permute-start | bytes 1572872 | tf_op jit(solution)/shard_map/ppermute | solution.py:41
  112.8 3.8 %collective-permute-start.13 = (f32[128,1024]{1,0:T(8,128)S(1)}, f32[128,1024]{1,0:T(8,128)S(1)}, u32[]{:S(2)}, u32[]{:S(2)}) collective-permute-start(f32[128,1024]{1,0:T(8,128)S(1)} %get-tuple-element.27), channel_id=1, source_target_pairs={{64,0},{65,1},{66,2},{67,3},{68,4},{69,5},{70,6},{71,7},{72,8},{73... | collective-permute-start | bytes 1572872 | tf_op jit(solution)/shard_map/ppermute | solution.py:41
  116.9 30.1 %copy-start.10 = (f32[128,1024]{1,0:T(8,128)}, f32[128,1024]{1,0:T(8,128)S(1)}, u32[]{:S(2)}) copy-start(f32[128,1024]{1,0:T(8,128)S(1)} %multiply_add_fusion.3) | copy-start | bytes 1572868
  116.9 3.6 %collective-permute-start.14 = (f32[1,128,1024]{2,1,0:T(8,128)S(1)}, f32[1,128,1024]{2,1,0:T(8,128)S(1)}, u32[]{:S(2)}, u32[]{:S(2)}) collective-permute-start(f32[1,128,1024]{2,1,0:T(8,128)S(1)} %bitcast.237), channel_id=1, source_target_pairs={{0,64},{1,65},{2,66},{3,67},{4,68},{5,69},{6,70},{7,71},{8,72},{9,... | collective-permute-start | bytes 1572872 | tf_op jit(solution)/shard_map/ppermute | solution.py:20
  122.6 24.4 %copy-start.15 = (f32[128,1024]{1,0:T(8,128)}, f32[128,1024]{1,0:T(8,128)S(1)}, u32[]{:S(2)}) copy-start(f32[128,1024]{1,0:T(8,128)S(1)} %get-tuple-element.25) | copy-start | bytes 1572868
  122.6 24.4 %copy-start.16 = (f32[128,1024]{1,0:T(8,128)}, f32[128,1024]{1,0:T(8,128)S(1)}, u32[]{:S(2)}) copy-start(f32[128,1024]{1,0:T(8,128)S(1)} %get-tuple-element.26) | copy-start | bytes 1572868
  122.6 24.4 %copy-start.24 = (f32[1,128,1024]{2,1,0:T(8,128)}, f32[1,128,1024]{2,1,0:T(8,128)S(1)}, u32[]{:S(2)}) copy-start(f32[1,128,1024]{2,1,0:T(8,128)S(1)} %get-tuple-element.24) | copy-start | bytes 1572868
  122.6 18.4 %collective-permute-start.15 = (f32[1,128,1024]{2,1,0:T(8,128)S(1)}, f32[1,128,1024]{2,1,0:T(8,128)S(1)}, u32[]{:S(2)}, u32[]{:S(2)}) collective-permute-start(f32[1,128,1024]{2,1,0:T(8,128)S(1)} %get-tuple-element.24), channel_id=1, source_target_pairs={{64,0},{65,1},{66,2},{67,3},{68,4},{69,5},{70,6},{71,7},{72,8},{73... | collective-permute-start | bytes 1572872 | tf_op jit(solution)/shard_map/ppermute | solution.py:21
  124.7 22.3 %copy-start.9 = (f32[4,128,1024]{2,1,0:T(8,128)S(1)}, f32[4,128,1024]{2,1,0:T(8,128)}, u32[]{:S(2)}) copy-start(f32[4,128,1024]{2,1,0:T(8,128)} %param.11) | copy-start | bytes 6291460
  125.5 21.4 %copy-start.3 = (f32[4,128,1024]{2,1,0:T(8,128)S(1)}, f32[4,128,1024]{2,1,0:T(8,128)}, u32[]{:S(2)}) copy-start(f32[4,128,1024]{2,1,0:T(8,128)} %param.7) | copy-start | bytes 6291460
  125.5 21.4 %copy-start.7 = (f32[3,128,1024]{2,1,0:T(8,128)S(1)}, f32[3,128,1024]{2,1,0:T(8,128)}, u32[]{:S(2)}) copy-start(f32[3,128,1024]{2,1,0:T(8,128)} %copy-done.6) | copy-start | bytes 4718596
  125.8 21.2 %copy-start.1 = (f32[4,128,1024]{2,1,0:T(8,128)S(1)}, f32[4,128,1024]{2,1,0:T(8,128)}, u32[]{:S(2)}) copy-start(f32[4,128,1024]{2,1,0:T(8,128)} %param.8) | copy-start | bytes 6291460
  125.8 15.1 %collective-permute-start.17 = (f32[4,1,1024]{2,1,0:T(1,128)S(1)}, f32[4,1,1024]{2,1,0:T(1,128)S(1)}, u32[]{:S(2)}, u32[]{:S(2)}) collective-permute-start(f32[4,1,1024]{2,1,0:T(1,128)S(1)} %get-tuple-element.50), channel_id=1, source_target_pairs={{0,4},{4,8},{8,12},{12,16},{16,20},{20,24},{24,28},{28,32},{32,36}... | collective-permute-start | bytes 49160 | tf_op jit(solution)/shard_map/ppermute | solution.py:20
  129.7 11.2 %collective-permute-start.16 = (f32[4,1,1024]{2,1,0:T(1,128)S(1)}, f32[4,1,1024]{2,1,0:T(1,128)S(1)}, u32[]{:S(2)}, u32[]{:S(2)}) collective-permute-start(f32[4,1,1024]{2,1,0:T(1,128)S(1)} %get-tuple-element.51), channel_id=1, source_target_pairs={{4,0},{8,4},{12,8},{16,12},{20,16},{24,20},{28,24},{32,28},{36,32}... | collective-permute-start | bytes 49160 | tf_op jit(solution)/shard_map/ppermute | solution.py:21
  135.1 10.7 %collective-permute-start.18 = (f32[4,128,1]{2,1,0:T(8,128)S(1)}, f32[4,128,1]{2,1,0:T(8,128)S(1)}, u32[]{:S(2)}, u32[]{:S(2)}) collective-permute-start(f32[4,128,1]{2,1,0:T(8,128)S(1)} %get-tuple-element.48), channel_id=1, source_target_pairs={{1,0},{2,1},{3,2},{5,4},{6,5},{7,6},{9,8},{10,9},{11,10},{13,12},{... | collective-permute-start | bytes 6152 | tf_op jit(solution)/shard_map/ppermute | solution.py:21
  136.4 10.6 %collective-permute-start.19 = (f32[4,128,1]{2,1,0:T(8,128)S(1)}, f32[4,128,1]{2,1,0:T(8,128)S(1)}, u32[]{:S(2)}, u32[]{:S(2)}) collective-permute-start(f32[4,128,1]{2,1,0:T(8,128)S(1)} %get-tuple-element.49), channel_id=1, source_target_pairs={{0,1},{1,2},{2,3},{4,5},{5,6},{6,7},{8,9},{9,10},{10,11},{12,13},{... | collective-permute-start | bytes 6152 | tf_op jit(solution)/shard_map/ppermute | solution.py:20
where the time goes:
time: 201 us
  blocking collectives  66.7 us (33%)
  starting transfers between devices  52.4 us (26%)
  other arithmetic  40.2 us (20%)
  waiting for transfers between devices  27.4 us (14%)
  between operations  7.53 us (4%)
  local copies, waits for them, and re-layouts  6.31 us (3%)
    psum x8, blocking collectives, by_axis(): value = lax.psum(value, axis)  66.7 us
    ppermute x6, starting transfers between devices, extended(): lax.ppermute(last, axis, up)  21.6 us
    reduce_sum x2, other arithmetic, paired_sums(): jnp.sum(image * precond)  20 us
    ppermute x8, starting transfers between devices, from_behind(): return lax.ppermute(value, axis, pairs)  17.2 us
    ppermute x8, waiting for transfers between devices, from_behind(): return lax.ppermute(value, axis, pairs)  13.9 us
    ppermute x6, starting transfers between devices, extended(): lax.ppermute(initial, axis, [(b, a) for a, b in up])  13.6 us
    sub x2, other arithmetic, shards(): residual = residual - alpha * along  8.84 us
    ppermute x6, waiting for transfers between devices, extended(): lax.ppermute(initial, axis, [(b, a) for a, b in up])  8.16 us
  transfers between devices with their start and end apart: 20, of which 12 were waited for; matrix products, arithmetic and copies ran while one was open for 2% of the time, Pallas kernels for 0%

commit v1 on v0

v1 whole, which is shorter than its diff:
```python
import functools

import jax
import jax.numpy as jnp
from jax import lax
from jax.experimental import pallas as pl
from jax.experimental.pallas import tpu as pltpu
from jax.sharding import PartitionSpec as P

MESH = pl.DeviceIdType.MESH
F32 = jnp.float32
D = 4
T = 8
W = 128


def kernel(
    shape, counts,
    b_hbm, rw_hbm, cl_hbm, vi_hbm, mk_hbm, gd_hbm,
    x_ref, r_ref,
    bb, rwp, cl, vi, mk, gd, inv, gain, num, w_ref, v_ref, c3, q3a, q3b,
    zb, qb, yb, qyb, fg_out, fg_in, f_out, f_in,
    row_out, row_in, col_out, col_in,
    zrow_out, zrow_in, zcol_out, zcol_in,
    part, group, total_out, total_in,
    load_sem, s_send, s_recv, z_send, z_recv, m_send, m_recv, g_send, g_recv, p_send, p_recv,
):
    rows, cols = shape
    layers, pxs, pys = counts
    nt = cols // W
    ni = rows // T
    layer = lax.axis_index("layer")
    px = lax.axis_index("px")
    py = lax.axis_index("py")
    bottom = layer == 0
    loc = [s + layer * (D - 1 - 2 * s) for s in range(D)]
    via = [s + layer * (D - 2 - 2 * s) for s in range(D - 1)]
    size1 = layers * pys
    me1 = layer * pys + py

    def group_peer(d):
        other = lax.rem(me1 + d, size1)
        return {"layer": other // pys, "py": lax.rem(other, pys)}

    def px_peer(d):
        return {"px": lax.rem(px + d, pxs)}

    def py_peer(d):
        return {"py": lax.rem(py + d, pys)}

    partner = {"layer": 1 - layer}
    barrier = pltpu.get_barrier_semaphore()
    for d in range(1, size1):
        pl.semaphore_signal(barrier, inc=1, device_id=group_peer(d), device_id_type=MESH)
    for d in range(1, pxs):
        pl.semaphore_signal(barrier, inc=1, device_id=px_peer(d), device_id_type=MESH)

    slot = [0]

    def load(src, dst):
        copy = pltpu.make_async_copy(src, dst, load_sem.at[slot[0]])
        slot[0] += 1
        copy.start()
        return copy

    last = (nt - 1) * W
    first_loads = [
        load(rw_hbm.at[:, rows - T : rows, :], rwp.at[:, rows : rows + T, :]),
        load(cl_hbm.at[:, :, last : last + W], cl.at[:, :, last : last + W]),
        load(vi_hbm.at[D - 1], vi.at[D - 1]),
        load(mk_hbm.at[D - 1], mk.at[D - 1]),
    ]
    chunks = 4
    step = rows // chunks
    chunk_loads = []
    for c in range(chunks):
        at = pl.ds(c * step, step)
        short = step - T if c == chunks - 1 else step
        chunk_loads.append([
            load(rw_hbm.at[:, pl.ds(c * step, short), :], rwp.at[:, pl.ds(T + c * step, short), :]),
            load(cl_hbm.at[:, at, 0:last], cl.at[:, at, 0:last]),
            load(vi_hbm.at[0 : D - 1, at, :], vi.at[0 : D - 1, at, :]),
            load(mk_hbm.at[0 : D - 1, at, :], mk.at[0 : D - 1, at, :]),
            load(gd_hbm.at[:, at, :], gd.at[:, at, :]),
            load(b_hbm.at[:, at, :], bb.at[:, at, :]),
        ])

    lane = lax.broadcasted_iota(jnp.int32, (T, W), 1)
    sub = lax.broadcasted_iota(jnp.int32, (T, W), 0)
    zero = jnp.zeros((T, W), F32)

    def remote(src, dst, send, recv, peer):
        return pltpu.make_async_remote_copy(
            src_ref=src, dst_ref=dst, send_sem=send, recv_sem=recv,
            device_id=peer, device_id_type=MESH,
        )

    def lanes(t):
        return slice(t * W, (t + 1) * W)

    def tile_at(r):
        return pl.ds(pl.multiple_of(r, T), T)

    for copy in first_loads:
        copy.wait()
    for s in range(D):
        for t in range(nt):
            row_out[s, t : t + 1, :] = rwp[loc[s], rows + T - 1 : rows + T, lanes(t)]

    def pack_col(i, packed):
        at = tile_at(i * T)
        for s in range(D):
            k = s * ni + i
            packed = jnp.where(lane == k, pltpu.roll(cl[loc[s], at, lanes(nt - 1)], k + 1, axis=1), packed)
        return packed

    col_out[...] = lax.fori_loop(0, ni, pack_col, zero)

    def join(i, carry):
        at = tile_at(i * T)
        c3[at, :] = vi[D - 1, at, :] * mk[D - 1, at, :].astype(F32)
        return carry

    @pl.when(bottom)
    def _():
        lax.fori_loop(0, ni, join, 0)

    pl.semaphore_wait(barrier, size1 - 1 + pxs - 1)
    row_copy = remote(row_out, row_in, s_send.at[0], s_recv.at[0], px_peer(1))
    col_copy = remote(col_out, col_in, s_send.at[1], s_recv.at[1], py_peer(1))
    row_copy.start()
    col_copy.start()
    c3_copy = remote(c3, c3, s_send.at[2], s_recv.at[2], partner)

    @pl.when(bottom)
    def _():
        c3_copy.start()

    sends = [row_copy, col_copy]

    def inner(i):
        r = i * T
        return [(r, t) for t in range(1, nt - 1)]

    def sides(j):
        starts = [j * 4 * T + m * T for m in range(4)]
        return [(r, t) for r in starts for t in (0, nt - 1)]

    def ends(j):
        r = j * (rows - T)
        return [(r, t) for t in range(1, nt - 1)]

    def edge_work(body, carry):
        carry = lax.fori_loop(0, ni // 4, lambda j, c: body(sides(j), c), carry)
        return lax.fori_loop(0, 2, lambda j, c: body(ends(j), c), carry)

    def inner_work(body, carry, start=1, stop=None):
        stop = ni - 1 if stop is None else stop
        return lax.fori_loop(start, stop, lambda i, c: body(inner(i), c), carry)

    def spread(packed, k, to):
        return pltpu.roll(packed, lax.rem(to + W - k, W), axis=1)

    def factor(items, carry):
        g = [None] * len(items)
        n = [None] * len(items)
        below = [None] * len(items)
        for s in range(D):
            l = loc[s]
            for m, (r, t) in enumerate(items):
                at = tile_at(r)
                rw = rwp[l, tile_at(r + T), lanes(t)]
                before = rwp[l, at, lanes(t)]
                up = pltpu.roll(jnp.where(sub == T - 1, before, rw), 1, axis=0)
                c = cl[l, at, lanes(t)]
                if t == 0:
                    k = s * ni + r // T
                    left = jnp.where(lane == 0, spread(col_in[...], k, 0), pltpu.roll(c, 1, axis=1))
                else:
                    left = pltpu.roll(jnp.where(lane == W - 1, cl[l, at, lanes(t - 1)], c), 1, axis=1)
                if s < D - 1:
                    above = vi[via[s], at, lanes(t)] * mk[via[s], at, lanes(t)].astype(F32)
                else:
                    above = c3[at, lanes(t)]
                diagonal = gd[l, at, lanes(t)] + rw + up + c + left + above
                right_side = bb[l, at, lanes(t)]
                if s:
                    diagonal = diagonal + below[m]
                    inverse = 1.0 / (diagonal - below[m] * g[m])
                    n[m] = right_side + g[m] * n[m]
                else:
                    inverse = 1.0 / diagonal
                    n[m] = right_side
                below[m] = above
                g[m] = above * inverse
                inv[s, at, lanes(t)] = inverse
                gain[s, at, lanes(t)] = g[m]
                num[s, at, lanes(t)] = n[m]
                if s == D - 1:
                    fg_out[0, at, lanes(t)] = n[m] * inverse
                    fg_out[1, at, lanes(t)] = g[m]
        return carry

    regions = [
        (pl.ds(T, rows - 2 * T), pl.ds(W, cols - 2 * W)),
        (pl.ds(0, rows), pl.ds(0, W)),
        (pl.ds(0, rows), pl.ds(cols - W, W)),
        (pl.ds(0, T), pl.ds(W, cols - 2 * W)),
        (pl.ds(rows - T, T), pl.ds(W, cols - 2 * W)),
    ]

    def middle(out, into, which, base):
        copies = []
        for e in which:
            i, j = regions[e]
            if len(out.shape) == 3:
                src, dst = out.at[:, i, j], into.at[:, i, j]
            else:
                src, dst = out.at[i, j], into.at[i, j]
            copies.append(remote(src, dst, m_send.at[base + e], m_recv.at[base + e], partner))
        for copy in copies:
            copy.start()
        sends.extend(copies)
        return copies

    @pl.when(jnp.logical_not(bottom))
    def _():
        c3_copy.wait_recv()

    for c in range(chunks):
        for copy in chunk_loads[c]:
            copy.wait()
        lo = max(1, c * step // T)
        hi = min(ni - 1, (c + 1) * step // T)
        inner_work(factor, 0, lo, hi)
    fg_inner = middle(fg_out, fg_in, [0], 0)

    row_copy.wait_recv()
    col_copy.wait_recv()
    has_upper = px > 0
    has_left = py > 0
    for s in range(D):
        for t in range(nt):
            rwp[loc[s], T - 1 : T, lanes(t)] = jnp.where(has_upper, row_in[s, t : t + 1, :], 0.0)
    col_in[...] = jnp.where(has_left, col_in[...], 0.0)
    edge_work(factor, 0)
    fg_edge = middle(fg_out, fg_in, [1, 2, 3, 4], 0)

    def solve(first, z, q, f_ref, items, carry):
        rho, pack_l, pack_r = carry
        following = [None] * len(items)
        terms = []
        for s in range(D - 1, -1, -1):
            l = loc[s]
            for m, (r, t) in enumerate(items):
                at = tile_at(r)
                if s == D - 1:
                    if first:
                        other = fg_in[1, at, lanes(t)]
                        g = gain[s, at, lanes(t)]
                        quotient = 1.0 / (1.0 - g * other)
                        scale = quotient * inv[s, at, lanes(t)]
                        g = quotient * g
                        q3a[at, lanes(t)] = scale
                        q3b[at, lanes(t)] = g
                        theirs = fg_in[0, at, lanes(t)]
                    else:
                        scale = q3a[at, lanes(t)]
                        g = q3b[at, lanes(t)]
                        theirs = f_ref[at, lanes(t)]
                    value = scale * num[s, at, lanes(t)] + g * theirs
                else:
                    value = num[s, at, lanes(t)] * inv[s, at, lanes(t)] + gain[s, at, lanes(t)] * following[m]
                following[m] = value
                z[s, t, tile_at(r + T), :] = value
                q[s, t, tile_at(r + T), :] = rwp[l, tile_at(r + T), lanes(t)] * value
                if first:
                    terms.append(bb[l, at, lanes(t)] * value)
                if t == 0:
                    k = s * ni + r // T
                    pack_l = jnp.where(lane == k, pltpu.roll(value, k, axis=1), pack_l)
                if t == nt - 1:
                    k = s * ni + r // T
                    side = cl[l, at, lanes(t)] * value
                    pack_r = jnp.where(lane == k, pltpu.roll(side, k + 1, axis=1), pack_r)
        if first:
            rho = rho + tree(terms)
        return rho, pack_l, pack_r

    def tree(values):
        while len(values) > 1:
            values = [a + b for a, b in zip(values[::2], values[1::2])] + ([values[-1]] if len(values) % 2 else [])
        return values[0]

    def halo_send(z, q, pack_l, pack_r, stage):
        zcol_out[stage, 0] = pack_l
        zcol_out[stage, 1] = pack_r
        for s in range(D):
            for t in range(nt):
                zrow_out[stage, 0, s, t : t + 1, :] = z[s, t, T : T + 1, :]
                zrow_out[stage, 1, s, t : t + 1, :] = q[s, t, rows + T - 1 : rows + T, :]
        copies = []
        for n, (out, into, peer) in enumerate((
            (zcol_out.at[stage, 0], zcol_in.at[stage, 0], py_peer(pys - 1)),
            (zcol_out.at[stage, 1], zcol_in.at[stage, 1], py_peer(1)),
            (zrow_out.at[stage, 0], zrow_in.at[stage, 0], px_peer(pxs - 1)),
            (zrow_out.at[stage, 1], zrow_in.at[stage, 1], px_peer(1)),
        )):
            copies.append(remote(out, into, z_send.at[4 * stage + n], z_recv.at[4 * stage + n], peer))
        for copy in copies:
            copy.start()
        sends.extend(copies)
        return copies

    def halo_wait(copies, z, q, stage):
        for copy in copies:
            copy.wait_recv()
        has_lower = px < pxs - 1
        has_right = py < pys - 1
        zcol_in[stage, 0] = jnp.where(has_right, zcol_in[stage, 0], 0.0)
        zcol_in[stage, 1] = jnp.where(has_left, zcol_in[stage, 1], 0.0)
        for s in range(D):
            for t in range(nt):
                z[s, t, rows + T : rows + T + 1, :] = jnp.where(has_lower, zrow_in[stage, 0, s, t : t + 1, :], 0.0)
                q[s, t, T - 1 : T, :] = jnp.where(has_upper, zrow_in[stage, 1, s, t : t + 1, :], 0.0)

    solve_z = functools.partial(solve, True, zb, qb, None)
    carry = (zero, zero, zero)
    for copy in fg_inner + fg_edge:
        copy.wait_recv()
    carry = edge_work(solve_z, carry)
    z_copies = halo_send(zb, qb, carry[1], carry[2], 0)
    rho_part = inner_work(solve_z, carry)[0]

    def coupled(z, q, stage, s, items):
        l = loc[s]
        zs, ps, out = {}, {}, []

        def own(m, r, t):
            if (m, t) not in zs:
                zs[m, t] = z[s, t, tile_at(r + T), :]
            return zs[m, t]

        def product(m, r, t):
            if (m, t) not in ps:
                ps[m, t] = cl[l, tile_at(r), lanes(t)] * own(m, r, t)
            return ps[m, t]

        rows_seen = []
        for r, t in items:
            m = next((n for n, other in enumerate(rows_seen) if other is r), None)
            if m is None:
                rows_seen.append(r)
                m = len(rows_seen) - 1
            at = tile_at(r)
            value = own(m, r, t)
            down = z[s, t, pl.ds(r + T + 1, T), :]
            up = q[s, t, pl.ds(r + T - 1, T), :]
            k = s * ni + r // T
            if t == nt - 1:
                right = jnp.where(lane == W - 1, spread(zcol_in[stage, 0], k, W - 1), pltpu.roll(value, W - 1, axis=1))
            else:
                right = pltpu.roll(jnp.where(lane == 0, own(m, r, t + 1), value), W - 1, axis=1)
            if t == 0:
                left = jnp.where(lane == 0, spread(zcol_in[stage, 1], k, 0), pltpu.roll(product(m, r, t), 1, axis=1))
            else:
                left = pltpu.roll(jnp.where(lane == W - 1, product(m, r, t - 1), product(m, r, t)), 1, axis=1)
            rw = rwp[l, tile_at(r + T), lanes(t)]
            c = cl[l, at, lanes(t)]
            out.append((value, rw * down + up + (c * right + left)))
        return out

    def apply_z(items, curve):
        n = [None] * len(items)
        terms = []
        for s in range(D):
            for m, ((r, t), (value, h)) in enumerate(zip(items, coupled(zb, qb, 0, s, items))):
                at = tile_at(r)
                w = bb[loc[s], at, lanes(t)] - h
                w_ref[s, at, lanes(t)] = w
                terms.append(value * w)
                n[m] = w if s == 0 else w + gain[s - 1, at, lanes(t)] * n[m]
                num[s, at, lanes(t)] = n[m]
                if s == D - 1:
                    f_out[at, lanes(t)] = n[m] * inv[s, at, lanes(t)]
        return curve + tree(terms)

    curve_part = inner_work(apply_z, zero)
    f_inner = middle(f_out, f_in, [0], 5)
    halo_wait(z_copies, zb, qb, 0)
    curve_part = edge_work(apply_z, curve_part)
    f_edge = middle(f_out, f_in, [1, 2, 3, 4], 5)

    def full(value):
        return jnp.sum(jnp.sum(value, axis=0, keepdims=True), axis=1, keepdims=True)

    row_lane = lax.broadcasted_iota(jnp.int32, (1, W), 1)

    def line(values):
        out = jnp.zeros((1, W), F32)
        for n, value in enumerate(values):
            out = jnp.where(row_lane == n, value, out)
        return out

    def gather_group(stage, values):
        part[stage] = line(values)
        group[stage, pl.ds(me1, 1)] = line(values)[None]
        copies = [
            remote(
                part.at[stage], group.at[stage, me1],
                g_send.at[stage * size1 + d], g_recv.at[stage * size1 + d], group_peer(d),
            )
            for d in range(1, size1)
        ]
        for copy in copies:
            copy.start()
        sends.extend(copies)
        return copies

    def group_sum(stage, copies):
        for copy in copies:
            copy.wait_recv()
        return tree([group[stage, m] for m in range(size1)])

    group_copies = gather_group(0, [full(rho_part), full(curve_part)])

    solve_y = functools.partial(solve, False, yb, qyb, f_in)
    carry = (zero, zero, zero)
    for copy in f_inner:
        copy.wait_recv()
    carry = inner_work(solve_y, carry)
    for copy in f_edge:
        copy.wait_recv()
    carry = edge_work(solve_y, carry)
    y_copies = halo_send(yb, qyb, carry[1], carry[2], 1)

    sums = group_sum(0, group_copies)

    def pick(value, n):
        return jnp.sum(jnp.where(row_lane == n, value, 0.0), axis=1, keepdims=True)

    rho_group, curve_group = pick(sums, 0), pick(sums, 1)
    ok = (rho_group > 0.0) & (curve_group > 0.0)
    centre = jnp.where(ok, rho_group / jnp.where(ok, curve_group, 1.0), 1.0)
    centre_tile = jnp.broadcast_to(centre, (T, W))

    def apply_y(items, acc):
        terms = [[] for _ in acc]
        for s in range(D):
            for (r, t), (y, h) in zip(items, coupled(yb, qyb, 1, s, items)):
                at = tile_at(r)
                w = w_ref[s, at, lanes(t)]
                v = w - h
                v_ref[s, at, lanes(t)] = v
                z = zb[s, t, tile_at(r + T), :]
                res = bb[loc[s], at, lanes(t)] - centre_tile * w
                pre = z - centre_tile * y
                image = w - centre_tile * v
                for n, term in enumerate((res * pre, w * y, pre * image, y * v, z * v)):
                    terms[n].append(term)
        return tuple(a + tree(b) for a, b in zip(acc, terms))

    acc = inner_work(apply_y, (zero,) * 5)
    halo_wait(y_copies, yb, qyb, 1)
    acc = edge_work(apply_y, acc)

    group_copies = gather_group(1, [full(a) for a in acc])
    sums2 = group_sum(1, group_copies)
    message = line([pick(sums2, n) for n in range(5)] + [centre, rho_group, curve_group])
    total_out[...] = message
    total_in[pl.ds(px, 1), :] = message
    copies = [
        remote(total_out, total_in.at[pl.ds(px, 1), :], p_send.at[d], p_recv.at[d], px_peer(d))
        for d in range(1, pxs)
    ]
    for copy in copies:
        copy.start()
    sends.extend(copies)
    for copy in copies:
        copy.wait_recv()
    table = total_in[...]
    table_lane = lax.broadcasted_iota(jnp.int32, table.shape, 1)
    s0, s2, t0, t2, zv, at0, rho_g, curve_g = (
        jnp.sum(jnp.where(table_lane == n, table, 0.0), axis=1, keepdims=True) for n in range(8)
    )

    def over(value):
        return jnp.sum(value, axis=0, keepdims=True)

    rho = over(rho_g)
    alpha = rho / over(curve_g)
    delta = jnp.broadcast_to(alpha, at0.shape) - at0
    rho_next = over(s0 - delta * (2.0 * (curve_g - at0 * s2) - delta * s2))
    curve = over(t0 - delta * ((s2 + zv - 2.0 * at0 * t2) - delta * t2))
    beta = rho_next / rho
    alpha_next = rho_next / (curve - beta * rho_next / alpha)
    big = jnp.broadcast_to(alpha + alpha_next * (1.0 + beta), (T, W))
    small = jnp.broadcast_to(alpha * alpha_next, (T, W))

    def finish(i, carry):
        at = tile_at(i * T)
        for s in range(D):
            l = loc[s]
            for t in range(nt):
                z = zb[s, t, tile_at(i * T + T), :]
                y = yb[s, t, tile_at(i * T + T), :]
                x_ref[l, at, lanes(t)] = big * z - small * y
                r_ref[l, at, lanes(t)] = bb[l, at, lanes(t)] - big * w_ref[s, at, lanes(t)] + small * v_ref[s, at, lanes(t)]
        return carry

    lax.fori_loop(0, ni, finish, 0)
    for copy in sends:
        copy.wait_send()

    @pl.when(bottom)
    def _():
        c3_copy.wait_send()


def solution(mesh):
    layers, pxs, pys = (mesh.shape[a] for a in ("layer", "px", "py"))
    spec = P("layer", "px", "py")

    def step(*args):
        depth, rows, cols = args[0].shape
        nt = cols // W
        block = (depth, rows, cols)
        padded = (depth, nt, rows + 2 * T, W)
        size1 = layers * pys
        dma = pltpu.SemaphoreType.DMA
        vmem = lambda *dims: pltpu.VMEM(dims, F32)
        scratch = [
            vmem(*block), vmem(depth, rows + T, cols), vmem(*block), vmem(*block),
            pltpu.VMEM(block, jnp.int32), vmem(*block), vmem(*block), vmem(*block), vmem(*block),
            vmem(*block), vmem(*block), vmem(rows, cols), vmem(rows, cols), vmem(rows, cols),
            vmem(*padded), vmem(*padded), vmem(*padded), vmem(*padded),
            vmem(2, rows, cols), vmem(2, rows, cols), vmem(rows, cols), vmem(rows, cols),
            vmem(depth, nt, W), vmem(depth, nt, W), vmem(T, W), vmem(T, W),
            vmem(2, 2, depth, nt, W), vmem(2, 2, depth, nt, W), vmem(2, 2, T, W), vmem(2, 2, T, W),
            vmem(2, 1, W), vmem(2, size1, 1, W), vmem(1, W), vmem(pxs, W),
            dma((28,)), dma((3,)), dma((3,)), dma((8,)), dma((8,)), dma((10,)), dma((10,)),
            dma((2 * size1,)), dma((2 * size1,)), dma((pxs,)), dma((pxs,)),
        ]
        out = jax.ShapeDtypeStruct(block, F32)
        return pl.pallas_call(
            functools.partial(kernel, (rows, cols), (layers, pxs, pys)),
            out_shape=(out, out),
            in_specs=[pl.BlockSpec(memory_space=pltpu.HBM)] * 6,
            out_specs=(pl.BlockSpec(memory_space=pltpu.VMEM),) * 2,
            scratch_shapes=scratch,
            compiler_params=pltpu.CompilerParams(
                collective_id=0, has_side_effects=True, vmem_limit_bytes=48 * 2**20
            ),
        )(*args)

    return jax.shard_map(step, mesh=mesh, in_specs=(spec,) * 6, out_specs=(spec, spec), check_vma=False)
```

time: 201 us -> 39.9 us (0.20)
  the two profiles are of different devices: /device:TPU:2 before, /device:TPU:1 now
where the time goes in v1:
time: 39.9 us; the launch traced here: 39.6 us
  Pallas kernels  36.3 us (91%)
  local copies, waits for them, and re-layouts  2.64 us (7%)
  between operations  0.64 us (2%)
    pallas_call x1, Pallas kernels, step(): pl.pallas_call(functools.partial(kernel, (rows, cols), (layers, pxs, pys)...  36.3 us
    unnamed x2, local copies, waits for them, and re-layouts  2.64 us

profile of v1, /device:TPU:1, one launch (start us, length us, event | category | flops | bytes accessed | tf_op | source)
XLA Modules:
  0.0 39.6 jit_solution(6062668985860194608)
XLA Ops:
  0.6 36.3 %shard_map.77 = (f32[4,128,1024]{2,1,0:T(8,128)S(1)}, f32[4,128,1024]{2,1,0:T(8,128)S(1)}) custom-call(f32[4,128,1024]{2,1,0:T(8,128)} %b_hbm.1, f32[4,128,1024]{2,1,0:T(8,128)} %rw_hbm.1, f32[4,128,1024]{2,1,0:T(8,128)} %cl_hbm.1, f32[4,128,1024]{2,1,0:T(8,128)} %vi_hbm.1, s32[4,128,1024]{2,1,0:T(8,128)} %mk_hbm.1, f32[4,128,1024]{2,1,0:T(8,128)} %gd_hbm.1), custom_call_target="tpu_custom_call" | custom-call | tf_op jit(solution)/shard_map/pallas_call | solution.py:545
  37.0 1.3 %copy.10 = f32[4,128,1024]{2,1,0:T(8,128)} copy(f32[4,128,1024]{2,1,0:T(8,128)S(1)} %get-tuple-element.4) | data formatting | bytes 4194304
  38.3 1.3 %copy.11 = f32[4,128,1024]{2,1,0:T(8,128)} copy(f32[4,128,1024]{2,1,0:T(8,128)S(1)} %get-tuple-element.5) | data formatting | bytes 4194304

commit v2 on v1

--- a/solution.py
+++ b/solution.py
@@ -17,13 +17,13 @@
 def kernel(
     shape, counts,
     b_hbm, rw_hbm, cl_hbm, vi_hbm, mk_hbm, gd_hbm,
-    x_ref, r_ref,
-    bb, rwp, cl, vi, mk, gd, inv, gain, num, w_ref, v_ref, c3, q3a, q3b,
-    zb, qb, yb, qyb, fg_out, fg_in, f_out, f_in,
+    bb, zb, yb, w_ref, v_ref, factors,
+    rwp, cl, vi, mk, gd, inv, gain, num, c3, q3a, q3b,
+    qb, qyb, fg_out, fg_in, f_out, f_in,
     row_out, row_in, col_out, col_in,
     zrow_out, zrow_in, zcol_out, zcol_in,
     part, group, total_out, total_in,
-    load_sem, s_send, s_recv, z_send, z_recv, m_send, m_recv, g_send, g_recv, p_send, p_recv,
+    load_sem, s_send, s_recv, z_send, z_recv, m_send, m_recv, g_send, g_recv, p_send, p_recv, far_sem,
 ):
     rows, cols = shape
     layers, pxs, pys = counts
@@ -49,27 +49,31 @@
         return {"py": lax.rem(py + d, pys)}
 
     partner = {"layer": 1 - layer}
-    barrier = pltpu.get_barrier_semaphore()
-    for d in range(1, size1):
-        pl.semaphore_signal(barrier, inc=1, device_id=group_peer(d), device_id_type=MESH)
-    for d in range(1, pxs):
-        pl.semaphore_signal(barrier, inc=1, device_id=px_peer(d), device_id_type=MESH)
+    near = [partner, px_peer(1), px_peer(pxs - 1), py_peer(1), py_peer(pys - 1)]
 
     slot = [0]
 
     def load(src, dst):
         copy = pltpu.make_async_copy(src, dst, load_sem.at[slot[0]])
         slot[0] += 1
-        copy.start()
         return copy
 
     last = (nt - 1) * W
-    first_loads = [
-        load(rw_hbm.at[:, rows - T : rows, :], rwp.at[:, rows : rows + T, :]),
-        load(cl_hbm.at[:, :, last : last + W], cl.at[:, :, last : last + W]),
-        load(vi_hbm.at[D - 1], vi.at[D - 1]),
-        load(mk_hbm.at[D - 1], mk.at[D - 1]),
-    ]
+    cl_edge = load(cl_hbm.at[:, :, last : last + W], cl.at[:, :, last : last + W])
+    rw_edge = load(rw_hbm.at[:, rows - T : rows, :], rwp.at[:, rows : rows + T, :])
+    top_loads = [load(vi_hbm.at[D - 1], vi.at[D - 1]), load(mk_hbm.at[D - 1], mk.at[D - 1])]
+    cl_edge.start()
+    rw_edge.start()
+
+    @pl.when(bottom)
+    def _():
+        for copy in top_loads:
+            copy.start()
+
+    barrier = pltpu.get_barrier_semaphore()
+    for peer in near:
+        pl.semaphore_signal(barrier, inc=1, device_id=peer, device_id_type=MESH)
+
     chunks = 4
     step = rows // chunks
     chunk_loads = []
@@ -84,6 +88,8 @@
             load(gd_hbm.at[:, at, :], gd.at[:, at, :]),
             load(b_hbm.at[:, at, :], bb.at[:, at, :]),
         ])
+        for copy in chunk_loads[-1]:
+            copy.start()
 
     lane = lax.broadcasted_iota(jnp.int32, (T, W), 1)
     sub = lax.broadcasted_iota(jnp.int32, (T, W), 0)
@@ -101,20 +107,30 @@
     def tile_at(r):
         return pl.ds(pl.multiple_of(r, T), T)
 
-    for copy in first_loads:
-        copy.wait()
+    cl_edge.wait()
+    packs = []
+    for s in range(D):
+        packed = zero
+        for i in range(ni):
+            k = s * ni + i
+            value = cl[loc[s], i * T : (i + 1) * T, lanes(nt - 1)]
+            packed = jnp.where(lane == k, pltpu.roll(value, (k + 1) % W, axis=1), packed)
+        packs.append(packed)
+    col_out[...] = (packs[0] + packs[1]) + (packs[2] + packs[3])
+    rw_edge.wait()
     for s in range(D):
         for t in range(nt):
             row_out[s, t : t + 1, :] = rwp[loc[s], rows + T - 1 : rows + T, lanes(t)]
 
-    def pack_col(i, packed):
-        at = tile_at(i * T)
-        for s in range(D):
-            k = s * ni + i
-            packed = jnp.where(lane == k, pltpu.roll(cl[loc[s], at, lanes(nt - 1)], k + 1, axis=1), packed)
-        return packed
-
-    col_out[...] = lax.fori_loop(0, ni, pack_col, zero)
+    pl.semaphore_wait(barrier, len(near))
+    row_copy = remote(row_out, row_in, s_send.at[0], s_recv.at[0], px_peer(1))
+    col_copy = remote(col_out, col_in, s_send.at[1], s_recv.at[1], py_peer(1))
+    col_copy.start()
+    row_copy.start()
+    c3_copies = [
+        remote(c3.at[pl.ds(c * step, step)], c3.at[pl.ds(c * step, step)], s_send.at[2 + c], s_recv.at[2 + c], partner)
+        for c in range(chunks)
+    ]
 
     def join(i, carry):
         at = tile_at(i * T)
@@ -123,18 +139,11 @@
 
     @pl.when(bottom)
     def _():
-        lax.fori_loop(0, ni, join, 0)
-
-    pl.semaphore_wait(barrier, size1 - 1 + pxs - 1)
-    row_copy = remote(row_out, row_in, s_send.at[0], s_recv.at[0], px_peer(1))
-    col_copy = remote(col_out, col_in, s_send.at[1], s_recv.at[1], py_peer(1))
-    row_copy.start()
-    col_copy.start()
-    c3_copy = remote(c3, c3, s_send.at[2], s_recv.at[2], partner)
-
-    @pl.when(bottom)
-    def _():
-        c3_copy.start()
+        for copy in top_loads:
+            copy.wait()
+        for c in range(chunks):
+            lax.fori_loop(c * step // T, (c + 1) * step // T, join, 0)
+            c3_copies[c].start()
 
     sends = [row_copy, col_copy]
 
@@ -223,13 +232,14 @@
         sends.extend(copies)
         return copies
 
-    @pl.when(jnp.logical_not(bottom))
-    def _():
-        c3_copy.wait_recv()
-
     for c in range(chunks):
         for copy in chunk_loads[c]:
             copy.wait()
+
+        @pl.when(jnp.logical_not(bottom))
+        def _():
+            c3_copies[c].wait_recv()
+
         lo = max(1, c * step // T)
         hi = min(ni - 1, (c + 1) * step // T)
         inner_work(factor, 0, lo, hi)
@@ -325,12 +335,13 @@
                 q[s, t, T - 1 : T, :] = jnp.where(has_upper, zrow_in[stage, 1, s, t : t + 1, :], 0.0)
 
     solve_z = functools.partial(solve, True, zb, qb, None)
-    carry = (zero, zero, zero)
-    for copy in fg_inner + fg_edge:
+    for copy in fg_inner:
         copy.wait_recv()
-    carry = edge_work(solve_z, carry)
-    z_copies = halo_send(zb, qb, carry[1], carry[2], 0)
-    rho_part = inner_work(solve_z, carry)[0]
+    rho_inner = inner_work(solve_z, (zero, zero, zero))[0]
+    for copy in fg_edge:
+        copy.wait_recv()
+    rho_edge, pack_l, pack_r = edge_work(solve_z, (zero, zero, zero))
+    z_copies = halo_send(zb, qb, pack_l, pack_r, 0)
 
     def coupled(z, q, stage, s, items):
         l = loc[s]
@@ -385,12 +396,6 @@
                     f_out[at, lanes(t)] = n[m] * inv[s, at, lanes(t)]
         return curve + tree(terms)
 
-    curve_part = inner_work(apply_z, zero)
-    f_inner = middle(f_out, f_in, [0], 5)
-    halo_wait(z_copies, zb, qb, 0)
-    curve_part = edge_work(apply_z, curve_part)
-    f_edge = middle(f_out, f_in, [1, 2, 3, 4], 5)
-
     def full(value):
         return jnp.sum(jnp.sum(value, axis=0, keepdims=True), axis=1, keepdims=True)
 
@@ -422,7 +427,23 @@
             copy.wait_recv()
         return tree([group[stage, m] for m in range(size1)])
 
-    group_copies = gather_group(0, [full(rho_part), full(curve_part)])
+    curve_inner = inner_work(apply_z, zero)
+    f_inner = middle(f_out, f_in, [0], 5)
+    group_copies = gather_group(0, [full(rho_inner), full(curve_inner)])
+    halo_wait(z_copies, zb, qb, 0)
+
+    hops = []
+    while (2 << len(hops)) * 2 < pxs:
+        hops.append(2 << len(hops))
+
+    def greet(n):
+        for d in (hops[n], pxs - hops[n]):
+            pl.semaphore_signal(far_sem.at[n], inc=1, device_id=px_peer(d), device_id_type=MESH)
+
+    if hops:
+        greet(0)
+    curve_edge = edge_work(apply_z, zero)
+    f_edge = middle(f_out, f_in, [1, 2, 3, 4], 5)
 
     solve_y = functools.partial(solve, False, yb, qyb, f_in)
     carry = (zero, zero, zero)
@@ -433,6 +454,10 @@
         copy.wait_recv()
     carry = edge_work(solve_y, carry)
     y_copies = halo_send(yb, qyb, carry[1], carry[2], 1)
+    if hops:
+        pl.semaphore_wait(far_sem.at[0], 2)
+        if len(hops) > 1:
+            greet(1)
 
     sums = group_sum(0, group_copies)
 
@@ -464,9 +489,19 @@
     halo_wait(y_copies, yb, qyb, 1)
     acc = edge_work(apply_y, acc)
 
-    group_copies = gather_group(1, [full(a) for a in acc])
-    sums2 = group_sum(1, group_copies)
-    message = line([pick(sums2, n) for n in range(5)] + [centre, rho_group, curve_group])
+    s0, s2, t0, t2, zv, rho_own, curve_own = (
+        full(value) for value in acc + (rho_inner + rho_edge, curve_inner + curve_edge)
+    )
+    group_copies = gather_group(1, [
+        s0, 2.0 * (curve_own - centre * s2), s2,
+        t0, s2 + zv - 2.0 * centre * t2, t2,
+        rho_own, curve_own,
+    ])
+    for n in range(1, len(hops)):
+        pl.semaphore_wait(far_sem.at[n], 2)
+        if n + 1 < len(hops):
+            greet(n + 1)
+    message = jnp.where(row_lane == 8, centre, group_sum(1, group_copies))
     total_out[...] = message
     total_in[pl.ds(px, 1), :] = message
     copies = [
@@ -480,41 +515,59 @@
         copy.wait_recv()
     table = total_in[...]
     table_lane = lax.broadcasted_iota(jnp.int32, table.shape, 1)
-    s0, s2, t0, t2, zv, at0, rho_g, curve_g = (
-        jnp.sum(jnp.where(table_lane == n, table, 0.0), axis=1, keepdims=True) for n in range(8)
-    )
-
-    def over(value):
-        return jnp.sum(value, axis=0, keepdims=True)
-
-    rho = over(rho_g)
-    alpha = rho / over(curve_g)
-    delta = jnp.broadcast_to(alpha, at0.shape) - at0
-    rho_next = over(s0 - delta * (2.0 * (curve_g - at0 * s2) - delta * s2))
-    curve = over(t0 - delta * ((s2 + zv - 2.0 * at0 * t2) - delta * t2))
+    centres = jnp.sum(jnp.where(table_lane == 8, table, 0.0), axis=1, keepdims=True)
+    plain = jnp.sum(table, axis=0, keepdims=True)
+    rho, curve_first = pick(plain, 6), pick(plain, 7)
+    alpha = rho / curve_first
+    delta = alpha - centres
+    linear = (table_lane == 1) | (table_lane == 4)
+    square = (table_lane == 2) | (table_lane == 5)
+    powers = jnp.where(linear, -delta, jnp.where(square, delta * delta, 1.0))
+    moved = jnp.sum(table * powers, axis=0, keepdims=True)
+    rho_next = jnp.sum(jnp.where(row_lane < 3, moved, 0.0), axis=1, keepdims=True)
+    curve = jnp.sum(jnp.where((row_lane >= 3) & (row_lane < 6), moved, 0.0), axis=1, keepdims=True)
     beta = rho_next / rho
     alpha_next = rho_next / (curve - beta * rho_next / alpha)
-    big = jnp.broadcast_to(alpha + alpha_next * (1.0 + beta), (T, W))
-    small = jnp.broadcast_to(alpha * alpha_next, (T, W))
-
-    def finish(i, carry):
-        at = tile_at(i * T)
+    factors[0] = jnp.broadcast_to(alpha + alpha_next * (1.0 + beta), (T, W))
+    factors[1] = jnp.broadcast_to(alpha * alpha_next, (T, W))
+    for copy in sends:
+        copy.wait_send()
+
+    @pl.when(bottom)
+    def _():
+        for copy in c3_copies:
+            copy.wait_send()
+
+
+def finish(shape, bb, zb, yb, w_ref, v_ref, factors, x_hbm, r_hbm, x_buf, r_buf, sem):
+    rows, cols = shape
+    layer = lax.axis_index("layer")
+    loc = [s + layer * (D - 1 - 2 * s) for s in range(D)]
+    big, small = factors[0], factors[1]
+    chunks = 4
+    step = rows // chunks
+    copies = []
+
+    def body(i, carry):
+        r = i * T
+        at = pl.ds(pl.multiple_of(r, T), T)
+        above = pl.ds(pl.multiple_of(r + T, T), T)
         for s in range(D):
             l = loc[s]
-            for t in range(nt):
-                z = zb[s, t, tile_at(i * T + T), :]
-                y = yb[s, t, tile_at(i * T + T), :]
-                x_ref[l, at, lanes(t)] = big * z - small * y
-                r_ref[l, at, lanes(t)] = bb[l, at, lanes(t)] - big * w_ref[s, at, lanes(t)] + small * v_ref[s, at, lanes(t)]
+            for t in range(cols // W):
+                col = slice(t * W, (t + 1) * W)
+                x_buf[l, at, col] = big * zb[s, t, above, :] - small * yb[s, t, above, :]
+                r_buf[l, at, col] = bb[l, at, col] - big * w_ref[s, at, col] + small * v_ref[s, at, col]
         return carry
 
-    lax.fori_loop(0, ni, finish, 0)
-    for copy in sends:
-        copy.wait_send()
-
-    @pl.when(bottom)
-    def _():
-        c3_copy.wait_send()
+    for c in range(chunks):
+        lax.fori_loop(c * step // T, (c + 1) * step // T, body, 0)
+        at = pl.ds(c * step, step)
+        for n, (src, dst) in enumerate(((x_buf, x_hbm), (r_buf, r_hbm))):
+            copies.append(pltpu.make_async_copy(src.at[:, at, :], dst.at[:, at, :], sem.at[2 * c + n]))
+            copies[-1].start()
+    for copy in copies:
+        copy.wait()
 
 
 def solution(mesh):
@@ -530,27 +583,36 @@
         dma = pltpu.SemaphoreType.DMA
         vmem = lambda *dims: pltpu.VMEM(dims, F32)
         scratch = [
-            vmem(*block), vmem(depth, rows + T, cols), vmem(*block), vmem(*block),
-            pltpu.VMEM(block, jnp.int32), vmem(*block), vmem(*block), vmem(*block), vmem(*block),
-            vmem(*block), vmem(*block), vmem(rows, cols), vmem(rows, cols), vmem(rows, cols),
-            vmem(*padded), vmem(*padded), vmem(*padded), vmem(*padded),
+            vmem(depth, rows + T, cols), vmem(*block), vmem(*block), pltpu.VMEM(block, jnp.int32), vmem(*block),
+            vmem(*block), vmem(*block), vmem(*block), vmem(rows, cols), vmem(rows, cols), vmem(rows, cols),
+            vmem(*padded), vmem(*padded),
             vmem(2, rows, cols), vmem(2, rows, cols), vmem(rows, cols), vmem(rows, cols),
             vmem(depth, nt, W), vmem(depth, nt, W), vmem(T, W), vmem(T, W),
             vmem(2, 2, depth, nt, W), vmem(2, 2, depth, nt, W), vmem(2, 2, T, W), vmem(2, 2, T, W),
             vmem(2, 1, W), vmem(2, size1, 1, W), vmem(1, W), vmem(pxs, W),
-            dma((28,)), dma((3,)), dma((3,)), dma((8,)), dma((8,)), dma((10,)), dma((10,)),
-            dma((2 * size1,)), dma((2 * size1,)), dma((pxs,)), dma((pxs,)),
+            dma((28,)), dma((6,)), dma((6,)), dma((8,)), dma((8,)), dma((10,)), dma((10,)),
+            dma((2 * size1,)), dma((2 * size1,)), dma((pxs,)), dma((pxs,)), pltpu.SemaphoreType.REGULAR((4,)),
         ]
-        out = jax.ShapeDtypeStruct(block, F32)
-        return pl.pallas_call(
+        out = lambda *dims: jax.ShapeDtypeStruct(dims, F32)
+        in_vmem = pl.BlockSpec(memory_space=pltpu.VMEM)
+        in_hbm = pl.BlockSpec(memory_space=pltpu.HBM)
+        kept = pl.pallas_call(
             functools.partial(kernel, (rows, cols), (layers, pxs, pys)),
-            out_shape=(out, out),
-            in_specs=[pl.BlockSpec(memory_space=pltpu.HBM)] * 6,
-            out_specs=(pl.BlockSpec(memory_space=pltpu.VMEM),) * 2,
+            out_shape=(vmem(*block), vmem(*padded), vmem(*padded), vmem(*block), vmem(*block), vmem(2, T, W)),
+            in_specs=[in_hbm] * 6,
+            out_specs=(in_vmem,) * 6,
             scratch_shapes=scratch,
             compiler_params=pltpu.CompilerParams(
-                collective_id=0, has_side_effects=True, vmem_limit_bytes=48 * 2**20
+                collective_id=0, has_side_effects=True, vmem_limit_bytes=36 * 2**20
             ),
-        )(*args)
+        )(*(pltpu.with_memory_space_constraint(arg, pltpu.HBM) for arg in args))
+        return pl.pallas_call(
+            functools.partial(finish, (rows, cols)),
+            out_shape=(out(*block), out(*block)),
+            in_specs=[in_vmem] * 6,
+            out_specs=(in_hbm, in_hbm),
+            scratch_shapes=[vmem(*block), vmem(*block), dma((8,))],
+            compiler_params=pltpu.CompilerParams(vmem_limit_bytes=6 * 2**20),
+        )(*kept)
 
     return jax.shard_map(step, mesh=mesh, in_specs=(spec,) * 6, out_specs=(spec, spec), check_vma=False)

time: 39.9 us -> 37.6 us (0.942)
  local copies, waits for them, and re-layouts: 2.64 us -> 0 us
  Pallas kernels: 36.3 us -> 36.7 us
    unnamed x2 -> x0, local copies, waits for them, and re-layouts: 2.64 us -> none
    pallas_call x0 -> x1, Pallas kernels: none -> 2.24 us  [step(): pl.pallas_call(functools.partial(finish, (rows, cols)), out_shape=(out(*b...]
    pallas_call x1, Pallas kernels: 36.3 us -> 34.4 us  [step(): pl.pallas_call(functools.partial(kernel, (rows, cols), (layers, pxs, pys)...]
where the time goes in v2:
time: 37.6 us; the launch traced here: 37.3 us
  Pallas kernels  36.7 us (98%)
  between operations  0.64 us (2%)
    pallas_call x1, Pallas kernels, step(): pl.pallas_call(functools.partial(kernel, (rows, cols), (layers, pxs, pys)...  34.4 us
    pallas_call x1, Pallas kernels, step(): pl.pallas_call(functools.partial(finish, (rows, cols)), out_shape=(out(*b...  2.24 us

profile of v2, /device:TPU:1, one launch (start us, length us, event | category | flops | bytes accessed | tf_op | source)
XLA Modules:
  0.0 37.3 jit_solution(14549383332578592372)
XLA Ops:
  0.6 34.4 %shard_map.77 = (f32[4,128,1024]{2,1,0:T(8,128)S(1)}, f32[4,8,144,128]{3,2,1,0:T(8,128)S(1)}, f32[4,8,144,128]{3,2,1,0:T(8,128)S(1)}, f32[4,128,1024]{2,1,0:T(8,...) custom-call(f32[4,128,1024]{2,1,0:T(8,128)} %b_hbm.1, f32[4,128,1024]{2,1,0:T(8,128)} %rw_hbm.1, ...), custom_call_target="tpu_custom_call" | custom-call | tf_op jit(solution)/shard_map/pallas_call | solution.py:599
  35.1 2.2 %shard_map.78 = (f32[4,128,1024]{2,1,0:T(8,128)}, f32[4,128,1024]{2,1,0:T(8,128)}) custom-call(f32[4,128,1024]{2,1,0:T(8,128)S(1)} %get-tuple-element.8.bb, f32[4,8,144,128]{3,2,1,0:T(8,128)S(1)} %get-tuple-element.9.zb, f32[4,8,144,128]{3,2,1,0:T(8,128)S(1)} %get-tuple-element.10.yb, f32[4,128,1024]{2,1,0:T(8,128)S(1)} %get-tuple-element.11.w_ref, ...), custom_call_target="tpu_custom_call" | custom-call | tf_op jit(solution)/shard_map/pallas_call | solution.py:609

commit v3 on v2

--- a/solution.py
+++ b/solution.py
@@ -14,7 +14,12 @@
 W = 128
 
 
-def kernel(
+def kernel(shape, counts, *refs):
+    dma = pltpu.SemaphoreType.DMA
+    pl.run_scoped(functools.partial(solve_all, shape, counts, *refs), dma((28,)), dma((32,)))
+
+
+def solve_all(
     shape, counts,
     b_hbm, rw_hbm, cl_hbm, vi_hbm, mk_hbm, gd_hbm,
     bb, zb, yb, w_ref, v_ref, factors,
@@ -22,8 +27,9 @@
     qb, qyb, fg_out, fg_in, f_out, f_in,
     row_out, row_in, col_out, col_in,
     zrow_out, zrow_in, zcol_out, zcol_in,
-    part, group, total_out, total_in,
-    load_sem, s_send, s_recv, z_send, z_recv, m_send, m_recv, g_send, g_recv, p_send, p_recv, far_sem,
+    part, group, total_out, table_ref, sized,
+    s_recv, z_recv, m_recv, g_recv, p_recv, far_sem,
+    load_sem, out_sem,
 ):
     rows, cols = shape
     layers, pxs, pys = counts
@@ -95,11 +101,19 @@
     sub = lax.broadcasted_iota(jnp.int32, (T, W), 0)
     zero = jnp.zeros((T, W), F32)
 
-    def remote(src, dst, send, recv, peer):
+    out_slot = [2]
+
+    def remote(src, dst, recv, peer, send=None):
+        if send is None:
+            send = out_sem.at[out_slot[0]]
+            out_slot[0] += 1
         return pltpu.make_async_remote_copy(
             src_ref=src, dst_ref=dst, send_sem=send, recv_sem=recv,
             device_id=peer, device_id_type=MESH,
         )
+
+    def wait_rows(count, sem):
+        pltpu.make_async_copy(sized.at[0:count], sized.at[0:count], sem).wait()
 
     def lanes(t):
         return slice(t * W, (t + 1) * W)
@@ -123,13 +137,17 @@
             row_out[s, t : t + 1, :] = rwp[loc[s], rows + T - 1 : rows + T, lanes(t)]
 
     pl.semaphore_wait(barrier, len(near))
-    row_copy = remote(row_out, row_in, s_send.at[0], s_recv.at[0], px_peer(1))
-    col_copy = remote(col_out, col_in, s_send.at[1], s_recv.at[1], py_peer(1))
+    row_copy = remote(row_out, row_in, s_recv.at[0], px_peer(1))
+    col_copy = remote(col_out, col_in, s_recv.at[1], py_peer(1))
     col_copy.start()
     row_copy.start()
+    for peer in near:
+        pl.semaphore_signal(far_sem.at[0], inc=1, device_id=peer, device_id_type=MESH)
+    pieces = 2
+    piece = rows // pieces
     c3_copies = [
-        remote(c3.at[pl.ds(c * step, step)], c3.at[pl.ds(c * step, step)], s_send.at[2 + c], s_recv.at[2 + c], partner)
-        for c in range(chunks)
+        remote(c3.at[pl.ds(c * piece, piece)], c3.at[pl.ds(c * piece, piece)], s_recv.at[2 + c], partner)
+        for c in range(pieces)
     ]
 
     def join(i, carry):
@@ -141,11 +159,24 @@
     def _():
         for copy in top_loads:
             copy.wait()
-        for c in range(chunks):
-            lax.fori_loop(c * step // T, (c + 1) * step // T, join, 0)
+        for c in range(pieces):
+            lax.fori_loop(c * piece // T, (c + 1) * piece // T, join, 0)
             c3_copies[c].start()
 
     sends = [row_copy, col_copy]
+
+    hops = []
+    while (2 << len(hops)) < pxs // 2:
+        hops.append(2 << len(hops))
+
+    def greet(n):
+        if n < len(hops):
+            for d in (hops[n], pxs - hops[n]):
+                pl.semaphore_signal(far_sem.at[1 + n], inc=1, device_id=px_peer(d), device_id_type=MESH)
+
+    def greeted(n):
+        if n < len(hops):
+            pl.semaphore_wait(far_sem.at[1 + n], 2)
 
     def inner(i):
         r = i * T
@@ -170,11 +201,20 @@
     def spread(packed, k, to):
         return pltpu.roll(packed, lax.rem(to + W - k, W), axis=1)
 
-    def factor(items, carry):
+    def coupling(s, at, t):
+        return vi[via[s], at, lanes(t)] * mk[via[s], at, lanes(t)].astype(F32)
+
+    def factor(first, stop, items, carry):
         g = [None] * len(items)
         n = [None] * len(items)
         below = [None] * len(items)
-        for s in range(D):
+        if first:
+            for m, (r, t) in enumerate(items):
+                at = tile_at(r)
+                g[m] = gain[first - 1, at, lanes(t)]
+                n[m] = num[first - 1, at, lanes(t)]
+                below[m] = coupling(first - 1, at, t)
+        for s in range(first, stop):
             l = loc[s]
             for m, (r, t) in enumerate(items):
                 at = tile_at(r)
@@ -188,7 +228,7 @@
                 else:
                     left = pltpu.roll(jnp.where(lane == W - 1, cl[l, at, lanes(t - 1)], c), 1, axis=1)
                 if s < D - 1:
-                    above = vi[via[s], at, lanes(t)] * mk[via[s], at, lanes(t)].astype(F32)
+                    above = coupling(s, at, t)
                 else:
                     above = c3[at, lanes(t)]
                 diagonal = gd[l, at, lanes(t)] + rw + up + c + left + above
@@ -220,31 +260,38 @@
 
     def middle(out, into, which, base):
         copies = []
-        for e in which:
-            i, j = regions[e]
+        for e, (i, j) in enumerate(which):
             if len(out.shape) == 3:
                 src, dst = out.at[:, i, j], into.at[:, i, j]
             else:
                 src, dst = out.at[i, j], into.at[i, j]
-            copies.append(remote(src, dst, m_send.at[base + e], m_recv.at[base + e], partner))
+            copies.append(remote(src, dst, m_recv.at[base + e], partner))
         for copy in copies:
             copy.start()
         sends.extend(copies)
         return copies
 
+    def deep(i):
+        r = i * T
+        return [(r, t) for t in range(1, nt)]
+
+    outer_levels = functools.partial(factor, 0, D - 1)
+    last_level = functools.partial(factor, D - 1, D)
+    all_levels = functools.partial(factor, 0, D)
     for c in range(chunks):
         for copy in chunk_loads[c]:
             copy.wait()
-
+        lax.fori_loop(max(1, c * step // T), (c + 1) * step // T, lambda i, x: outer_levels(deep(i), x), 0)
+    for c in range(pieces):
         @pl.when(jnp.logical_not(bottom))
         def _():
             c3_copies[c].wait_recv()
 
-        lo = max(1, c * step // T)
-        hi = min(ni - 1, (c + 1) * step // T)
-        inner_work(factor, 0, lo, hi)
-    fg_inner = middle(fg_out, fg_in, [0], 0)
-
+        lax.fori_loop(max(1, c * piece // T), (c + 1) * piece // T, lambda i, x: last_level(deep(i), x), 0)
+    fg_inner = middle(fg_out, fg_in, [(pl.ds(T, rows - T), pl.ds(W, cols - W))], 0)
+
+    pl.semaphore_wait(far_sem.at[0], len(near))
+    greet(0)
     row_copy.wait_recv()
     col_copy.wait_recv()
     has_upper = px > 0
@@ -253,8 +300,13 @@
         for t in range(nt):
             rwp[loc[s], T - 1 : T, lanes(t)] = jnp.where(has_upper, row_in[s, t : t + 1, :], 0.0)
     col_in[...] = jnp.where(has_left, col_in[...], 0.0)
-    edge_work(factor, 0)
-    fg_edge = middle(fg_out, fg_in, [1, 2, 3, 4], 0)
+    group_of = min(8, ni)
+    lax.fori_loop(
+        0, ni // group_of,
+        lambda j, x: all_levels([(j * group_of * T + m * T, 0) for m in range(group_of)], x), 0,
+    )
+    lax.fori_loop(0, 1, lambda i, x: all_levels(deep(i), x), 0)
+    fg_edge = middle(fg_out, fg_in, [(pl.ds(0, rows), pl.ds(0, W)), (pl.ds(0, T), pl.ds(W, cols - W))], 1)
 
     def solve(first, z, q, f_ref, items, carry):
         rho, pack_l, pack_r = carry
@@ -316,7 +368,7 @@
             (zrow_out.at[stage, 0], zrow_in.at[stage, 0], px_peer(pxs - 1)),
             (zrow_out.at[stage, 1], zrow_in.at[stage, 1], px_peer(1)),
         )):
-            copies.append(remote(out, into, z_send.at[4 * stage + n], z_recv.at[4 * stage + n], peer))
+            copies.append(remote(out, into, z_recv.at[4 * stage + n], peer))
         for copy in copies:
             copy.start()
         sends.extend(copies)
@@ -338,6 +390,8 @@
     for copy in fg_inner:
         copy.wait_recv()
     rho_inner = inner_work(solve_z, (zero, zero, zero))[0]
+    greeted(0)
+    greet(1)
     for copy in fg_edge:
         copy.wait_recv()
     rho_edge, pack_l, pack_r = edge_work(solve_z, (zero, zero, zero))
@@ -407,43 +461,26 @@
             out = jnp.where(row_lane == n, value, out)
         return out
 
-    def gather_group(stage, values):
-        part[stage] = line(values)
-        group[stage, pl.ds(me1, 1)] = line(values)[None]
-        copies = [
-            remote(
-                part.at[stage], group.at[stage, me1],
-                g_send.at[stage * size1 + d], g_recv.at[stage * size1 + d], group_peer(d),
-            )
-            for d in range(1, size1)
-        ]
-        for copy in copies:
-            copy.start()
-        sends.extend(copies)
-        return copies
-
-    def group_sum(stage, copies):
-        for copy in copies:
-            copy.wait_recv()
-        return tree([group[stage, m] for m in range(size1)])
+    def gather_group(values):
+        part[0] = line(values)
+        group[pl.ds(me1, 1)] = line(values)[None]
+        for d in range(1, size1):
+            remote(part.at[0], group.at[me1], g_recv, group_peer(d), out_sem.at[0]).start()
+
+    def group_sum():
+        wait_rows(size1 - 1, g_recv)
+        return tree([group[m] for m in range(size1)])
 
     curve_inner = inner_work(apply_z, zero)
-    f_inner = middle(f_out, f_in, [0], 5)
-    group_copies = gather_group(0, [full(rho_inner), full(curve_inner)])
+    f_inner = middle(f_out, f_in, regions[:1], 3)
+    for n in range(1, len(hops)):
+        greeted(n)
+        greet(n + 1)
+    gather_group([full(rho_inner), full(curve_inner)])
     halo_wait(z_copies, zb, qb, 0)
 
-    hops = []
-    while (2 << len(hops)) * 2 < pxs:
-        hops.append(2 << len(hops))
-
-    def greet(n):
-        for d in (hops[n], pxs - hops[n]):
-            pl.semaphore_signal(far_sem.at[n], inc=1, device_id=px_peer(d), device_id_type=MESH)
-
-    if hops:
-        greet(0)
     curve_edge = edge_work(apply_z, zero)
-    f_edge = middle(f_out, f_in, [1, 2, 3, 4], 5)
+    f_edge = middle(f_out, f_in, regions[1:], 4)
 
     solve_y = functools.partial(solve, False, yb, qyb, f_in)
     carry = (zero, zero, zero)
@@ -454,12 +491,8 @@
         copy.wait_recv()
     carry = edge_work(solve_y, carry)
     y_copies = halo_send(yb, qyb, carry[1], carry[2], 1)
-    if hops:
-        pl.semaphore_wait(far_sem.at[0], 2)
-        if len(hops) > 1:
-            greet(1)
-
-    sums = group_sum(0, group_copies)
+
+    sums = group_sum()
 
     def pick(value, n):
         return jnp.sum(jnp.where(row_lane == n, value, 0.0), axis=1, keepdims=True)
@@ -492,28 +525,30 @@
     s0, s2, t0, t2, zv, rho_own, curve_own = (
         full(value) for value in acc + (rho_inner + rho_edge, curve_inner + curve_edge)
     )
-    group_copies = gather_group(1, [
+    total_out[...] = line([
         s0, 2.0 * (curve_own - centre * s2), s2,
         t0, s2 + zv - 2.0 * centre * t2, t2,
-        rho_own, curve_own,
+        rho_own, curve_own, centre,
     ])
-    for n in range(1, len(hops)):
-        pl.semaphore_wait(far_sem.at[n], 2)
-        if n + 1 < len(hops):
-            greet(n + 1)
-    message = jnp.where(row_lane == 8, centre, group_sum(1, group_copies))
-    total_out[...] = message
-    total_in[pl.ds(px, 1), :] = message
-    copies = [
-        remote(total_out, total_in.at[pl.ds(px, 1), :], p_send.at[d], p_recv.at[d], px_peer(d))
-        for d in range(1, pxs)
+    mine = table_ref.at[pl.ds((layer * pxs + px) * pys + py, 1), :]
+    pz = 4 if pxs % 4 == 0 else pxs
+    px_hi = pxs // pz
+    there = [
+        (a, x, z, y) for a in range(layers) for x in range(px_hi) for z in range(pz) for y in range(pys)
     ]
-    for copy in copies:
-        copy.start()
-    sends.extend(copies)
-    for copy in copies:
-        copy.wait_recv()
-    table = total_in[...]
+    ring = lambda d, n: min(d, n - d)
+    there.sort(key=lambda o: -(ring(o[1], px_hi) + ring(o[2], pz) + ring(o[3], pys)))
+    for a, x, z, y in there:
+        if a or x or z or y:
+            peer = {
+                "layer": lax.rem(layer + a, layers),
+                "px": lax.rem(px // pz + x, px_hi) * pz + lax.rem(lax.rem(px, pz) + z, pz),
+                "py": lax.rem(py + y, pys),
+            }
+            remote(total_out, mine, p_recv, peer, out_sem.at[1]).start()
+    pltpu.make_async_copy(total_out, mine, p_recv).start()
+    pltpu.make_async_copy(table_ref, table_ref, p_recv).wait()
+    table = table_ref[...]
     table_lane = lax.broadcasted_iota(jnp.int32, table.shape, 1)
     centres = jnp.sum(jnp.where(table_lane == 8, table, 0.0), axis=1, keepdims=True)
     plain = jnp.sum(table, axis=0, keepdims=True)
@@ -532,6 +567,8 @@
     factors[1] = jnp.broadcast_to(alpha * alpha_next, (T, W))
     for copy in sends:
         copy.wait_send()
+    wait_rows(size1 - 1, out_sem.at[0])
+    wait_rows(len(there) - 1, out_sem.at[1])
 
     @pl.when(bottom)
     def _():
@@ -589,9 +626,8 @@
             vmem(2, rows, cols), vmem(2, rows, cols), vmem(rows, cols), vmem(rows, cols),
             vmem(depth, nt, W), vmem(depth, nt, W), vmem(T, W), vmem(T, W),
             vmem(2, 2, depth, nt, W), vmem(2, 2, depth, nt, W), vmem(2, 2, T, W), vmem(2, 2, T, W),
-            vmem(2, 1, W), vmem(2, size1, 1, W), vmem(1, W), vmem(pxs, W),
-            dma((28,)), dma((6,)), dma((6,)), dma((8,)), dma((8,)), dma((10,)), dma((10,)),
-            dma((2 * size1,)), dma((2 * size1,)), dma((pxs,)), dma((pxs,)), pltpu.SemaphoreType.REGULAR((4,)),
+            vmem(1, 1, W), vmem(size1, 1, W), vmem(1, W), vmem(size1 * pxs, W), vmem(size1 * pxs, 1, W),
+            dma((4,)), dma((8,)), dma((8,)), dma, dma, pltpu.SemaphoreType.REGULAR((4,)),
         ]
         out = lambda *dims: jax.ShapeDtypeStruct(dims, F32)
         in_vmem = pl.BlockSpec(memory_space=pltpu.VMEM)

time: 37.6 us -> 37 us (0.984)
  Pallas kernels: 36.7 us -> 36.2 us
    pallas_call x1, Pallas kernels: 34.4 us -> 34 us  [step(): pl.pallas_call(functools.partial(kernel, (rows, cols), (layers, pxs, pys)...]
where the time goes in v3:
time: 37 us; the launch traced here: 36.9 us
  Pallas kernels  36.2 us (98%)
  between operations  0.64 us (2%)
    pallas_call x1, Pallas kernels, step(): pl.pallas_call(functools.partial(kernel, (rows, cols), (layers, pxs, pys)...  34 us
    pallas_call x1, Pallas kernels, step(): pl.pallas_call(functools.partial(finish, (rows, cols)), out_shape=(out(*b...  2.24 us

profile of v3, /device:TPU:1, one launch (start us, length us, event | category | flops | bytes accessed | tf_op | source)
XLA Modules:
  0.0 36.9 jit_solution(2667953343165432730)
XLA Ops:
  0.6 34.0 %shard_map.77 = (f32[4,128,1024]{2,1,0:T(8,128)S(1)}, f32[4,8,144,128]{3,2,1,0:T(8,128)S(1)}, f32[4,8,144,128]{3,2,1,0:T(8,128)S(1)}, f32[4,128,1024]{2,1,0:T(8,...) custom-call(f32[4,128,1024]{2,1,0:T(8,128)} %refs_0_.1, f32[4,128,1024]{2,1,0:T(8,128)} %refs_1_.1, ...), custom_call_target="tpu_custom_call" | custom-call | tf_op jit(solution)/shard_map/pallas_call | solution.py:635
  34.6 2.2 %shard_map.78 = (f32[4,128,1024]{2,1,0:T(8,128)}, f32[4,128,1024]{2,1,0:T(8,128)}) custom-call(f32[4,128,1024]{2,1,0:T(8,128)S(1)} %get-tuple-element.8.bb, f32[4,8,144,128]{3,2,1,0:T(8,128)S(1)} %get-tuple-element.9.zb, f32[4,8,144,128]{3,2,1,0:T(8,128)S(1)} %get-tuple-element.10.yb, f32[4,128,1024]{2,1,0:T(8,128)S(1)} %get-tuple-element.11.w_ref, ...), custom_call_target="tpu_custom_call" | custom-call | tf_op jit(solution)/shard_map/pallas_call | solution.py:645

commit v4 on v3

--- a/solution.py
+++ b/solution.py
@@ -57,6 +57,12 @@
     partner = {"layer": 1 - layer}
     near = [partner, px_peer(1), px_peer(pxs - 1), py_peer(1), py_peer(pys - 1)]
 
+    barrier = pltpu.get_barrier_semaphore()
+    for peer in near:
+        pl.semaphore_signal(barrier, inc=1, device_id=peer, device_id_type=MESH)
+    has_upper, has_lower = px > 0, px < pxs - 1
+    has_left, has_right = py > 0, py < pys - 1
+
     slot = [0]
 
     def load(src, dst):
@@ -75,10 +81,6 @@
     def _():
         for copy in top_loads:
             copy.start()
-
-    barrier = pltpu.get_barrier_semaphore()
-    for peer in near:
-        pl.semaphore_signal(barrier, inc=1, device_id=peer, device_id_type=MESH)
 
     chunks = 4
     step = rows // chunks
@@ -101,6 +103,12 @@
     sub = lax.broadcasted_iota(jnp.int32, (T, W), 0)
     zero = jnp.zeros((T, W), F32)
 
+    def gate(condition, *actions):
+        @pl.when(condition)
+        def _():
+            for action in actions:
+                action()
+
     out_slot = [2]
 
     def remote(src, dst, recv, peer, send=None):
@@ -139,8 +147,8 @@
     pl.semaphore_wait(barrier, len(near))
     row_copy = remote(row_out, row_in, s_recv.at[0], px_peer(1))
     col_copy = remote(col_out, col_in, s_recv.at[1], py_peer(1))
-    col_copy.start()
-    row_copy.start()
+    gate(has_right, col_copy.start)
+    gate(has_lower, row_copy.start)
     for peer in near:
         pl.semaphore_signal(far_sem.at[0], inc=1, device_id=peer, device_id_type=MESH)
     pieces = 2
@@ -163,7 +171,8 @@
             lax.fori_loop(c * piece // T, (c + 1) * piece // T, join, 0)
             c3_copies[c].start()
 
-    sends = [row_copy, col_copy]
+    gated = [(has_lower, row_copy), (has_right, col_copy)]
+    sends = []
 
     hops = []
     while (2 << len(hops)) < pxs // 2:
@@ -278,24 +287,31 @@
     outer_levels = functools.partial(factor, 0, D - 1)
     last_level = functools.partial(factor, D - 1, D)
     all_levels = functools.partial(factor, 0, D)
-    for c in range(chunks):
+    fg_inner = []
+
+    def outer_part(c):
         for copy in chunk_loads[c]:
             copy.wait()
         lax.fori_loop(max(1, c * step // T), (c + 1) * step // T, lambda i, x: outer_levels(deep(i), x), 0)
-    for c in range(pieces):
-        @pl.when(jnp.logical_not(bottom))
-        def _():
-            c3_copies[c].wait_recv()
-
-        lax.fori_loop(max(1, c * piece // T), (c + 1) * piece // T, lambda i, x: last_level(deep(i), x), 0)
-    fg_inner = middle(fg_out, fg_in, [(pl.ds(T, rows - T), pl.ds(W, cols - W))], 0)
+
+    def last_part(c):
+        if c * step % piece == 0:
+            gate(jnp.logical_not(bottom), c3_copies[c * step // piece].wait_recv)
+        lo = max(T, c * step)
+        lax.fori_loop(lo // T, (c + 1) * step // T, lambda i, x: last_level(deep(i), x), 0)
+        fg_inner.append(middle(fg_out, fg_in, [(pl.ds(lo, (c + 1) * step - lo), pl.ds(W, cols - W))], c)[0])
+
+    for c in range(chunks):
+        outer_part(c)
+        if c >= chunks // 2:
+            last_part(c - chunks // 2)
+    for c in range(chunks // 2, chunks):
+        last_part(c)
 
     pl.semaphore_wait(far_sem.at[0], len(near))
     greet(0)
-    row_copy.wait_recv()
-    col_copy.wait_recv()
-    has_upper = px > 0
-    has_left = py > 0
+    gate(has_left, col_copy.wait_recv)
+    gate(has_upper, row_copy.wait_recv)
     for s in range(D):
         for t in range(nt):
             rwp[loc[s], T - 1 : T, lanes(t)] = jnp.where(has_upper, row_in[s, t : t + 1, :], 0.0)
@@ -306,7 +322,7 @@
         lambda j, x: all_levels([(j * group_of * T + m * T, 0) for m in range(group_of)], x), 0,
     )
     lax.fori_loop(0, 1, lambda i, x: all_levels(deep(i), x), 0)
-    fg_edge = middle(fg_out, fg_in, [(pl.ds(0, rows), pl.ds(0, W)), (pl.ds(0, T), pl.ds(W, cols - W))], 1)
+    fg_edge = middle(fg_out, fg_in, [(pl.ds(0, rows), pl.ds(0, W)), (pl.ds(0, T), pl.ds(W, cols - W))], 4)
 
     def solve(first, z, q, f_ref, items, carry):
         rho, pack_l, pack_r = carry
@@ -361,30 +377,33 @@
             for t in range(nt):
                 zrow_out[stage, 0, s, t : t + 1, :] = z[s, t, T : T + 1, :]
                 zrow_out[stage, 1, s, t : t + 1, :] = q[s, t, rows + T - 1 : rows + T, :]
-        copies = []
-        for n, (out, into, peer) in enumerate((
-            (zcol_out.at[stage, 0], zcol_in.at[stage, 0], py_peer(pys - 1)),
-            (zcol_out.at[stage, 1], zcol_in.at[stage, 1], py_peer(1)),
-            (zrow_out.at[stage, 0], zrow_in.at[stage, 0], px_peer(pxs - 1)),
-            (zrow_out.at[stage, 1], zrow_in.at[stage, 1], px_peer(1)),
-        )):
-            copies.append(remote(out, into, z_recv.at[4 * stage + n], peer))
-        for copy in copies:
-            copy.start()
-        sends.extend(copies)
+        copies = [
+            remote(out, into, z_recv.at[4 * stage + n], peer)
+            for n, (out, into, peer) in enumerate((
+                (zcol_out.at[stage, 0], zcol_in.at[stage, 0], py_peer(pys - 1)),
+                (zcol_out.at[stage, 1], zcol_in.at[stage, 1], py_peer(1)),
+                (zrow_out.at[stage, 0], zrow_in.at[stage, 0], px_peer(pxs - 1)),
+                (zrow_out.at[stage, 1], zrow_in.at[stage, 1], px_peer(1)),
+            ))
+        ]
+        for condition, copy in zip((has_upper, has_lower, has_left, has_right), copies[2:] + copies[:2]):
+            gate(condition, copy.start)
+            gated.append((condition, copy))
         return copies
 
-    def halo_wait(copies, z, q, stage):
-        for copy in copies:
-            copy.wait_recv()
-        has_lower = px < pxs - 1
-        has_right = py < pys - 1
+    def halo_wait(copies, stage):
+        for condition, copy in zip((has_right, has_left, has_lower, has_upper), copies):
+            gate(condition, copy.wait_recv)
         zcol_in[stage, 0] = jnp.where(has_right, zcol_in[stage, 0], 0.0)
         zcol_in[stage, 1] = jnp.where(has_left, zcol_in[stage, 1], 0.0)
+        zrow_in[stage, 0] = jnp.where(has_lower, zrow_in[stage, 0], 0.0)
+        zrow_in[stage, 1] = jnp.where(has_upper, zrow_in[stage, 1], 0.0)
+
+    def place_rows(z, q, stage):
         for s in range(D):
             for t in range(nt):
-                z[s, t, rows + T : rows + T + 1, :] = jnp.where(has_lower, zrow_in[stage, 0, s, t : t + 1, :], 0.0)
-                q[s, t, T - 1 : T, :] = jnp.where(has_upper, zrow_in[stage, 1, s, t : t + 1, :], 0.0)
+                z[s, t, rows + T : rows + T + 1, :] = zrow_in[stage, 0, s, t : t + 1, :]
+                q[s, t, T - 1 : T, :] = zrow_in[stage, 1, s, t : t + 1, :]
 
     solve_z = functools.partial(solve, True, zb, qb, None)
     for copy in fg_inner:
@@ -422,11 +441,15 @@
             down = z[s, t, pl.ds(r + T + 1, T), :]
             up = q[s, t, pl.ds(r + T - 1, T), :]
             k = s * ni + r // T
-            if t == nt - 1:
+            if t == nt - 1 and stage is None:
+                right = pltpu.roll(jnp.where(lane == 0, 0.0, value), W - 1, axis=1)
+            elif t == nt - 1:
                 right = jnp.where(lane == W - 1, spread(zcol_in[stage, 0], k, W - 1), pltpu.roll(value, W - 1, axis=1))
             else:
                 right = pltpu.roll(jnp.where(lane == 0, own(m, r, t + 1), value), W - 1, axis=1)
-            if t == 0:
+            if t == 0 and stage is None:
+                left = pltpu.roll(jnp.where(lane == W - 1, 0.0, product(m, r, t)), 1, axis=1)
+            elif t == 0:
                 left = jnp.where(lane == 0, spread(zcol_in[stage, 1], k, 0), pltpu.roll(product(m, r, t), 1, axis=1))
             else:
                 left = pltpu.roll(jnp.where(lane == W - 1, product(m, r, t - 1), product(m, r, t)), 1, axis=1)
@@ -450,8 +473,11 @@
                     f_out[at, lanes(t)] = n[m] * inv[s, at, lanes(t)]
         return curve + tree(terms)
 
+    def down(value):
+        return jnp.sum(value, axis=0, keepdims=True)
+
     def full(value):
-        return jnp.sum(jnp.sum(value, axis=0, keepdims=True), axis=1, keepdims=True)
+        return jnp.sum(down(value), axis=1, keepdims=True)
 
     row_lane = lax.broadcasted_iota(jnp.int32, (1, W), 1)
 
@@ -472,15 +498,16 @@
         return tree([group[m] for m in range(size1)])
 
     curve_inner = inner_work(apply_z, zero)
-    f_inner = middle(f_out, f_in, regions[:1], 3)
+    f_inner = middle(f_out, f_in, regions[:1], 6)
     for n in range(1, len(hops)):
         greeted(n)
         greet(n + 1)
     gather_group([full(rho_inner), full(curve_inner)])
-    halo_wait(z_copies, zb, qb, 0)
+    halo_wait(z_copies, 0)
+    place_rows(zb, qb, 0)
 
     curve_edge = edge_work(apply_z, zero)
-    f_edge = middle(f_out, f_in, regions[1:], 4)
+    f_edge = middle(f_out, f_in, regions[1:], 7)
 
     solve_y = functools.partial(solve, False, yb, qyb, f_in)
     carry = (zero, zero, zero)
@@ -505,7 +532,7 @@
     def apply_y(items, acc):
         terms = [[] for _ in acc]
         for s in range(D):
-            for (r, t), (y, h) in zip(items, coupled(yb, qyb, 1, s, items)):
+            for (r, t), (y, h) in zip(items, coupled(yb, qyb, None, s, items)):
                 at = tile_at(r)
                 w = w_ref[s, at, lanes(t)]
                 v = w - h
@@ -518,9 +545,26 @@
                     terms[n].append(term)
         return tuple(a + tree(b) for a, b in zip(acc, terms))
 
-    acc = inner_work(apply_y, (zero,) * 5)
-    halo_wait(y_copies, yb, qyb, 1)
-    acc = edge_work(apply_y, acc)
+    for s in range(D):
+        for t in range(nt):
+            yb[s, t, rows + T : rows + 2 * T, :] = zero
+            qyb[s, t, 0:T, :] = zero
+
+    def whole(i):
+        r = i * T
+        return [(r, t) for t in range(nt)]
+
+    acc = lax.fori_loop(0, ni, lambda i, c: apply_y(whole(i), c), (zero,) * 5)
+    halo_wait(y_copies, 1)
+
+    def edge_sums(stage):
+        cols_part = tree([zcol_out[stage, n] * zcol_in[1, 1 - n] for n in range(2)])
+        rows_part = tree([zrow_out[stage, n, s] * zrow_in[1, 1 - n, s] for n in range(2) for s in range(D)])
+        return down(cols_part) + down(rows_part)
+
+    edge_y, edge_z = edge_sums(1), edge_sums(0)
+    acc = tuple(down(a) for a in acc)
+    acc = (acc[0], acc[1], acc[2] + centre * (edge_z - centre * edge_y), acc[3] - edge_y, acc[4] - edge_z)
 
     s0, s2, t0, t2, zv, rho_own, curve_own = (
         full(value) for value in acc + (rho_inner + rho_edge, curve_inner + curve_edge)
@@ -547,6 +591,25 @@
             }
             remote(total_out, mine, p_recv, peer, out_sem.at[1]).start()
     pltpu.make_async_copy(total_out, mine, p_recv).start()
+    for s in range(D):
+        for t in range(nt):
+            v_ref[s, 0:1, lanes(t)] = v_ref[s, 0:1, lanes(t)] - zrow_in[1, 1, s, t : t + 1, :]
+            v_ref[s, rows - 1 : rows, lanes(t)] = (
+                v_ref[s, rows - 1 : rows, lanes(t)] - row_out[s, t : t + 1, :] * zrow_in[1, 0, s, t : t + 1, :]
+            )
+    right_part = col_out[...] * zcol_in[1, 0]
+    left_part = zcol_in[1, 1]
+
+    def mend(i, carry):
+        at = tile_at(i * T)
+        for s in range(D):
+            k = s * ni + i
+            first, final = lanes(0), lanes(nt - 1)
+            v_ref[s, at, first] = v_ref[s, at, first] - jnp.where(lane == 0, spread(left_part, k, 0), 0.0)
+            v_ref[s, at, final] = v_ref[s, at, final] - jnp.where(lane == W - 1, spread(right_part, k, W - 1), 0.0)
+        return carry
+
+    lax.fori_loop(0, ni, mend, 0)
     pltpu.make_async_copy(table_ref, table_ref, p_recv).wait()
     table = table_ref[...]
     table_lane = lax.broadcasted_iota(jnp.int32, table.shape, 1)
@@ -567,6 +630,8 @@
     factors[1] = jnp.broadcast_to(alpha * alpha_next, (T, W))
     for copy in sends:
         copy.wait_send()
+    for condition, copy in gated:
+        gate(condition, copy.wait_send)
     wait_rows(size1 - 1, out_sem.at[0])
     wait_rows(len(there) - 1, out_sem.at[1])
 
@@ -581,8 +646,7 @@
     layer = lax.axis_index("layer")
     loc = [s + layer * (D - 1 - 2 * s) for s in range(D)]
     big, small = factors[0], factors[1]
-    chunks = 4
-    step = rows // chunks
+    stops = [0, T, rows // 4, rows // 2, 3 * rows // 4, rows]
     copies = []
 
     def body(i, carry):
@@ -597,9 +661,11 @@
                 r_buf[l, at, col] = bb[l, at, col] - big * w_ref[s, at, col] + small * v_ref[s, at, col]
         return carry
 
-    for c in range(chunks):
-        lax.fori_loop(c * step // T, (c + 1) * step // T, body, 0)
-        at = pl.ds(c * step, step)
+    for c, (lo, hi) in enumerate(zip(stops, stops[1:])):
+        if hi == lo:
+            continue
+        lax.fori_loop(lo // T, hi // T, body, 0)
+        at = pl.ds(lo, hi - lo)
         for n, (src, dst) in enumerate(((x_buf, x_hbm), (r_buf, r_hbm))):
             copies.append(pltpu.make_async_copy(src.at[:, at, :], dst.at[:, at, :], sem.at[2 * c + n]))
             copies[-1].start()
@@ -627,7 +693,7 @@
             vmem(depth, nt, W), vmem(depth, nt, W), vmem(T, W), vmem(T, W),
             vmem(2, 2, depth, nt, W), vmem(2, 2, depth, nt, W), vmem(2, 2, T, W), vmem(2, 2, T, W),
             vmem(1, 1, W), vmem(size1, 1, W), vmem(1, W), vmem(size1 * pxs, W), vmem(size1 * pxs, 1, W),
-            dma((4,)), dma((8,)), dma((8,)), dma, dma, pltpu.SemaphoreType.REGULAR((4,)),
+            dma((4,)), dma((8,)), dma((11,)), dma, dma, pltpu.SemaphoreType.REGULAR((4,)),
         ]
         out = lambda *dims: jax.ShapeDtypeStruct(dims, F32)
         in_vmem = pl.BlockSpec(memory_space=pltpu.VMEM)
@@ -647,7 +713,7 @@
             out_shape=(out(*block), out(*block)),
             in_specs=[in_vmem] * 6,
             out_specs=(in_hbm, in_hbm),
-            scratch_shapes=[vmem(*block), vmem(*block), dma((8,))],
+            scratch_shapes=[vmem(*block), vmem(*block), dma((10,))],
             compiler_params=pltpu.CompilerParams(vmem_limit_bytes=6 * 2**20),
         )(*kept)
 

time: 37 us -> 33.7 us (0.911)
  Pallas kernels: 36.2 us -> 32.9 us
    pallas_call x1, Pallas kernels: 34 us -> 30.8 us  [step(): pl.pallas_call(functools.partial(kernel, (rows, cols), (layers, pxs, pys)...]
where the time goes in v4:
time: 33.7 us; the launch traced here: 33.6 us
  Pallas kernels  32.9 us (98%)
  between operations  0.64 us (2%)
    pallas_call x1, Pallas kernels, step(): pl.pallas_call(functools.partial(kernel, (rows, cols), (layers, pxs, pys)...  30.8 us
    pallas_call x1, Pallas kernels, step(): pl.pallas_call(functools.partial(finish, (rows, cols)), out_shape=(out(*b...  2.16 us

profile of v4, /device:TPU:1, one launch (start us, length us, event | category | flops | bytes accessed | tf_op | source)
XLA Modules:
  0.0 33.6 jit_solution(18417476198077967689)
XLA Ops:
  0.6 30.8 %shard_map.77 = (f32[4,128,1024]{2,1,0:T(8,128)S(1)}, f32[4,8,144,128]{3,2,1,0:T(8,128)S(1)}, f32[4,8,144,128]{3,2,1,0:T(8,128)S(1)}, f32[4,128,1024]{2,1,0:T(8,...) custom-call(f32[4,128,1024]{2,1,0:T(8,128)} %refs_0_.1, f32[4,128,1024]{2,1,0:T(8,128)} %refs_1_.1, ...), custom_call_target="tpu_custom_call" | custom-call | tf_op jit(solution)/shard_map/pallas_call | solution.py:701
  31.4 2.2 %shard_map.78 = (f32[4,128,1024]{2,1,0:T(8,128)}, f32[4,128,1024]{2,1,0:T(8,128)}) custom-call(f32[4,128,1024]{2,1,0:T(8,128)S(1)} %get-tuple-element.8.bb, f32[4,8,144,128]{3,2,1,0:T(8,128)S(1)} %get-tuple-element.9.zb, f32[4,8,144,128]{3,2,1,0:T(8,128)S(1)} %get-tuple-element.10.yb, f32[4,128,1024]{2,1,0:T(8,128)S(1)} %get-tuple-element.11.w_ref, ...), custom_call_target="tpu_custom_call" | custom-call | tf_op jit(solution)/shard_map/pallas_call | solution.py:711

commit v5 on v4

--- a/solution.py
+++ b/solution.py
@@ -28,7 +28,7 @@
     row_out, row_in, col_out, col_in,
     zrow_out, zrow_in, zcol_out, zcol_in,
     part, group, total_out, table_ref, sized,
-    s_recv, z_recv, m_recv, g_recv, p_recv, far_sem,
+    s_recv, z_recv, m_recv, g_recv, p_recv, far_sem, met_sem,
     load_sem, out_sem,
 ):
     rows, cols = shape
@@ -151,7 +151,7 @@
     gate(has_lower, row_copy.start)
     for peer in near:
         pl.semaphore_signal(far_sem.at[0], inc=1, device_id=peer, device_id_type=MESH)
-    pieces = 2
+    pieces = chunks
     piece = rows // pieces
     c3_copies = [
         remote(c3.at[pl.ds(c * piece, piece)], c3.at[pl.ds(c * piece, piece)], s_recv.at[2 + c], partner)
@@ -213,17 +213,11 @@
     def coupling(s, at, t):
         return vi[via[s], at, lanes(t)] * mk[via[s], at, lanes(t)].astype(F32)
 
-    def factor(first, stop, items, carry):
+    def factor(items, carry):
         g = [None] * len(items)
         n = [None] * len(items)
         below = [None] * len(items)
-        if first:
-            for m, (r, t) in enumerate(items):
-                at = tile_at(r)
-                g[m] = gain[first - 1, at, lanes(t)]
-                n[m] = num[first - 1, at, lanes(t)]
-                below[m] = coupling(first - 1, at, t)
-        for s in range(first, stop):
+        for s in range(D):
             l = loc[s]
             for m, (r, t) in enumerate(items):
                 at = tile_at(r)
@@ -284,29 +278,14 @@
         r = i * T
         return [(r, t) for t in range(1, nt)]
 
-    outer_levels = functools.partial(factor, 0, D - 1)
-    last_level = functools.partial(factor, D - 1, D)
-    all_levels = functools.partial(factor, 0, D)
     fg_inner = []
-
-    def outer_part(c):
+    for c in range(chunks):
         for copy in chunk_loads[c]:
             copy.wait()
-        lax.fori_loop(max(1, c * step // T), (c + 1) * step // T, lambda i, x: outer_levels(deep(i), x), 0)
-
-    def last_part(c):
-        if c * step % piece == 0:
-            gate(jnp.logical_not(bottom), c3_copies[c * step // piece].wait_recv)
-        lo = max(T, c * step)
-        lax.fori_loop(lo // T, (c + 1) * step // T, lambda i, x: last_level(deep(i), x), 0)
-        fg_inner.append(middle(fg_out, fg_in, [(pl.ds(lo, (c + 1) * step - lo), pl.ds(W, cols - W))], c)[0])
-
-    for c in range(chunks):
-        outer_part(c)
-        if c >= chunks // 2:
-            last_part(c - chunks // 2)
-    for c in range(chunks // 2, chunks):
-        last_part(c)
+        gate(jnp.logical_not(bottom), c3_copies[c].wait_recv)
+        lo, hi = max(T, c * step), (c + 1) * step
+        lax.fori_loop(lo // T, hi // T, lambda i, x: factor(deep(i), x), 0)
+        fg_inner += middle(fg_out, fg_in, [(pl.ds(lo, hi - lo), pl.ds(W, cols - W))], c)
 
     pl.semaphore_wait(far_sem.at[0], len(near))
     greet(0)
@@ -319,9 +298,9 @@
     group_of = min(8, ni)
     lax.fori_loop(
         0, ni // group_of,
-        lambda j, x: all_levels([(j * group_of * T + m * T, 0) for m in range(group_of)], x), 0,
+        lambda j, x: factor([(j * group_of * T + m * T, 0) for m in range(group_of)], x), 0,
     )
-    lax.fori_loop(0, 1, lambda i, x: all_levels(deep(i), x), 0)
+    lax.fori_loop(0, 1, lambda i, x: factor(deep(i), x), 0)
     fg_edge = middle(fg_out, fg_in, [(pl.ds(0, rows), pl.ds(0, W)), (pl.ds(0, T), pl.ds(W, cols - W))], 4)
 
     def solve(first, z, q, f_ref, items, carry):
@@ -409,8 +388,6 @@
     for copy in fg_inner:
         copy.wait_recv()
     rho_inner = inner_work(solve_z, (zero, zero, zero))[0]
-    greeted(0)
-    greet(1)
     for copy in fg_edge:
         copy.wait_recv()
     rho_edge, pack_l, pack_r = edge_work(solve_z, (zero, zero, zero))
@@ -499,15 +476,19 @@
 
     curve_inner = inner_work(apply_z, zero)
     f_inner = middle(f_out, f_in, regions[:1], 6)
+    greeted(0)
+    greet(1)
+    gather_group([full(rho_inner), full(curve_inner)])
+    halo_wait(z_copies, 0)
+    place_rows(zb, qb, 0)
+
+    curve_edge = edge_work(apply_z, zero)
+    f_edge = middle(f_out, f_in, regions[1:], 7)
     for n in range(1, len(hops)):
         greeted(n)
         greet(n + 1)
-    gather_group([full(rho_inner), full(curve_inner)])
-    halo_wait(z_copies, 0)
-    place_rows(zb, qb, 0)
-
-    curve_edge = edge_work(apply_z, zero)
-    f_edge = middle(f_out, f_in, regions[1:], 7)
+    for d in range(1, size1):
+        pl.semaphore_signal(met_sem, inc=1, device_id=group_peer(d), device_id_type=MESH)
 
     solve_y = functools.partial(solve, False, yb, qyb, f_in)
     carry = (zero, zero, zero)
@@ -574,6 +555,7 @@
         t0, s2 + zv - 2.0 * centre * t2, t2,
         rho_own, curve_own, centre,
     ])
+    pl.semaphore_wait(met_sem, size1 - 1)
     mine = table_ref.at[pl.ds((layer * pxs + px) * pys + py, 1), :]
     pz = 4 if pxs % 4 == 0 else pxs
     px_hi = pxs // pz
@@ -693,7 +675,7 @@
             vmem(depth, nt, W), vmem(depth, nt, W), vmem(T, W), vmem(T, W),
             vmem(2, 2, depth, nt, W), vmem(2, 2, depth, nt, W), vmem(2, 2, T, W), vmem(2, 2, T, W),
             vmem(1, 1, W), vmem(size1, 1, W), vmem(1, W), vmem(size1 * pxs, W), vmem(size1 * pxs, 1, W),
-            dma((4,)), dma((8,)), dma((11,)), dma, dma, pltpu.SemaphoreType.REGULAR((4,)),
+            dma((6,)), dma((8,)), dma((11,)), dma, dma, pltpu.SemaphoreType.REGULAR((4,)), pltpu.SemaphoreType.REGULAR,
         ]
         out = lambda *dims: jax.ShapeDtypeStruct(dims, F32)
         in_vmem = pl.BlockSpec(memory_space=pltpu.VMEM)

time: 33.7 us -> 32.7 us (0.970)
  Pallas kernels: 32.9 us -> 31.9 us
    pallas_call x1, Pallas kernels: 30.8 us -> 29.8 us  [step(): pl.pallas_call(functools.partial(kernel, (rows, cols), (layers, pxs, pys)...]
where the time goes in v5:
time: 32.7 us; the launch traced here: 32.6 us
  Pallas kernels  31.9 us (98%)
  between operations  0.64 us (2%)
    pallas_call x1, Pallas kernels, step(): pl.pallas_call(functools.partial(kernel, (rows, cols), (layers, pxs, pys)...  29.8 us
    pallas_call x1, Pallas kernels, step(): pl.pallas_call(functools.partial(finish, (rows, cols)), out_shape=(out(*b...  2.16 us

profile of v5, /device:TPU:1, one launch (start us, length us, event | category | flops | bytes accessed | tf_op | source)
XLA Modules:
  0.0 32.6 jit_solution(16730604565548716469)
XLA Ops:
  0.6 29.8 %shard_map.77 = (f32[4,128,1024]{2,1,0:T(8,128)S(1)}, f32[4,8,144,128]{3,2,1,0:T(8,128)S(1)}, f32[4,8,144,128]{3,2,1,0:T(8,128)S(1)}, f32[4,128,1024]{2,1,0:T(8,...) custom-call(f32[4,128,1024]{2,1,0:T(8,128)} %refs_0_.1, f32[4,128,1024]{2,1,0:T(8,128)} %refs_1_.1, ...), custom_call_target="tpu_custom_call" | custom-call | tf_op jit(solution)/shard_map/pallas_call | solution.py:683
  30.4 2.2 %shard_map.78 = (f32[4,128,1024]{2,1,0:T(8,128)}, f32[4,128,1024]{2,1,0:T(8,128)}) custom-call(f32[4,128,1024]{2,1,0:T(8,128)S(1)} %get-tuple-element.8.bb, f32[4,8,144,128]{3,2,1,0:T(8,128)S(1)} %get-tuple-element.9.zb, f32[4,8,144,128]{3,2,1,0:T(8,128)S(1)} %get-tuple-element.10.yb, f32[4,128,1024]{2,1,0:T(8,128)S(1)} %get-tuple-element.11.w_ref, ...), custom_call_target="tpu_custom_call" | custom-call | tf_op jit(solution)/shard_map/pallas_call | solution.py:693

commit v6 on v5

--- a/solution.py
+++ b/solution.py
@@ -191,17 +191,21 @@
         r = i * T
         return [(r, t) for t in range(1, nt - 1)]
 
+    span = 7 if (ni - 2) % 7 == 0 else 2
+
     def sides(j):
-        starts = [j * 4 * T + m * T for m in range(4)]
+        starts = [(1 + j * span + m) * T for m in range(span)]
         return [(r, t) for r in starts for t in (0, nt - 1)]
 
     def ends(j):
         r = j * (rows - T)
-        return [(r, t) for t in range(1, nt - 1)]
-
-    def edge_work(body, carry):
-        carry = lax.fori_loop(0, ni // 4, lambda j, c: body(sides(j), c), carry)
+        return [(r, t) for t in range(nt)]
+
+    def ends_work(body, carry):
         return lax.fori_loop(0, 2, lambda j, c: body(ends(j), c), carry)
+
+    def sides_work(body, carry):
+        return lax.fori_loop(0, (ni - 2) // span, lambda j, c: body(sides(j), c), carry)
 
     def inner_work(body, carry, start=1, stop=None):
         stop = ni - 1 if stop is None else stop
@@ -349,40 +353,59 @@
             values = [a + b for a, b in zip(values[::2], values[1::2])] + ([values[-1]] if len(values) % 2 else [])
         return values[0]
 
-    def halo_send(z, q, pack_l, pack_r, stage):
-        zcol_out[stage, 0] = pack_l
-        zcol_out[stage, 1] = pack_r
+    def start_halos(stage, first, pairs):
+        copies = []
+        for n, (condition, out, into, peer) in enumerate(pairs):
+            copy = remote(out, into, z_recv.at[4 * stage + first + n], peer)
+            gate(condition, copy.start)
+            gated.append((condition, copy))
+            copies.append(copy)
+        return copies
+
+    def send_rows(z, q, stage):
         for s in range(D):
             for t in range(nt):
                 zrow_out[stage, 0, s, t : t + 1, :] = z[s, t, T : T + 1, :]
                 zrow_out[stage, 1, s, t : t + 1, :] = q[s, t, rows + T - 1 : rows + T, :]
-        copies = [
-            remote(out, into, z_recv.at[4 * stage + n], peer)
-            for n, (out, into, peer) in enumerate((
-                (zcol_out.at[stage, 0], zcol_in.at[stage, 0], py_peer(pys - 1)),
-                (zcol_out.at[stage, 1], zcol_in.at[stage, 1], py_peer(1)),
-                (zrow_out.at[stage, 0], zrow_in.at[stage, 0], px_peer(pxs - 1)),
-                (zrow_out.at[stage, 1], zrow_in.at[stage, 1], px_peer(1)),
-            ))
-        ]
-        for condition, copy in zip((has_upper, has_lower, has_left, has_right), copies[2:] + copies[:2]):
-            gate(condition, copy.start)
-            gated.append((condition, copy))
-        return copies
+        return start_halos(stage, 0, (
+            (has_upper, zrow_out.at[stage, 0], zrow_in.at[stage, 0], px_peer(pxs - 1)),
+            (has_lower, zrow_out.at[stage, 1], zrow_in.at[stage, 1], px_peer(1)),
+        ))
+
+    def send_cols(pack_l, pack_r, stage):
+        zcol_out[stage, 0] = pack_l
+        zcol_out[stage, 1] = pack_r
+        return start_halos(stage, 2, (
+            (has_left, zcol_out.at[stage, 0], zcol_in.at[stage, 0], py_peer(pys - 1)),
+            (has_right, zcol_out.at[stage, 1], zcol_in.at[stage, 1], py_peer(1)),
+        ))
 
     def halo_wait(copies, stage):
-        for condition, copy in zip((has_right, has_left, has_lower, has_upper), copies):
+        for condition, copy in zip((has_lower, has_upper, has_right, has_left), copies):
             gate(condition, copy.wait_recv)
         zcol_in[stage, 0] = jnp.where(has_right, zcol_in[stage, 0], 0.0)
         zcol_in[stage, 1] = jnp.where(has_left, zcol_in[stage, 1], 0.0)
         zrow_in[stage, 0] = jnp.where(has_lower, zrow_in[stage, 0], 0.0)
         zrow_in[stage, 1] = jnp.where(has_upper, zrow_in[stage, 1], 0.0)
 
-    def place_rows(z, q, stage):
+    def mend_rows(ref, stage):
         for s in range(D):
             for t in range(nt):
-                z[s, t, rows + T : rows + T + 1, :] = zrow_in[stage, 0, s, t : t + 1, :]
-                q[s, t, T - 1 : T, :] = zrow_in[stage, 1, s, t : t + 1, :]
+                ref[s, 0:1, lanes(t)] = ref[s, 0:1, lanes(t)] - zrow_in[stage, 1, s, t : t + 1, :]
+                ref[s, rows - 1 : rows, lanes(t)] = (
+                    ref[s, rows - 1 : rows, lanes(t)] - row_out[s, t : t + 1, :] * zrow_in[stage, 0, s, t : t + 1, :]
+                )
+
+    def col_term(left_part, right_part, k, t):
+        if t == 0:
+            return jnp.where(lane == 0, spread(left_part, k, 0), 0.0)
+        return jnp.where(lane == W - 1, spread(right_part, k, W - 1), 0.0)
+
+    for z, q in ((zb, qb), (yb, qyb)):
+        for s in range(D):
+            for t in range(nt):
+                z[s, t, rows + T : rows + 2 * T, :] = zero
+                q[s, t, 0:T, :] = zero
 
     solve_z = functools.partial(solve, True, zb, qb, None)
     for copy in fg_inner:
@@ -390,10 +413,12 @@
     rho_inner = inner_work(solve_z, (zero, zero, zero))[0]
     for copy in fg_edge:
         copy.wait_recv()
-    rho_edge, pack_l, pack_r = edge_work(solve_z, (zero, zero, zero))
-    z_copies = halo_send(zb, qb, pack_l, pack_r, 0)
-
-    def coupled(z, q, stage, s, items):
+    carry = ends_work(solve_z, (zero, zero, zero))
+    z_copies = send_rows(zb, qb, 0)
+    rho_edge, pack_l, pack_r = sides_work(solve_z, carry)
+    z_copies += send_cols(pack_l, pack_r, 0)
+
+    def coupled(z, q, s, items):
         l = loc[s]
         zs, ps, out = {}, {}, []
 
@@ -417,19 +442,10 @@
             value = own(m, r, t)
             down = z[s, t, pl.ds(r + T + 1, T), :]
             up = q[s, t, pl.ds(r + T - 1, T), :]
-            k = s * ni + r // T
-            if t == nt - 1 and stage is None:
-                right = pltpu.roll(jnp.where(lane == 0, 0.0, value), W - 1, axis=1)
-            elif t == nt - 1:
-                right = jnp.where(lane == W - 1, spread(zcol_in[stage, 0], k, W - 1), pltpu.roll(value, W - 1, axis=1))
-            else:
-                right = pltpu.roll(jnp.where(lane == 0, own(m, r, t + 1), value), W - 1, axis=1)
-            if t == 0 and stage is None:
-                left = pltpu.roll(jnp.where(lane == W - 1, 0.0, product(m, r, t)), 1, axis=1)
-            elif t == 0:
-                left = jnp.where(lane == 0, spread(zcol_in[stage, 1], k, 0), pltpu.roll(product(m, r, t), 1, axis=1))
-            else:
-                left = pltpu.roll(jnp.where(lane == W - 1, product(m, r, t - 1), product(m, r, t)), 1, axis=1)
+            after = own(m, r, t + 1) if t < nt - 1 else 0.0
+            before = product(m, r, t - 1) if t else 0.0
+            right = pltpu.roll(jnp.where(lane == 0, after, value), W - 1, axis=1)
+            left = pltpu.roll(jnp.where(lane == W - 1, before, product(m, r, t)), 1, axis=1)
             rw = rwp[l, tile_at(r + T), lanes(t)]
             c = cl[l, at, lanes(t)]
             out.append((value, rw * down + up + (c * right + left)))
@@ -439,7 +455,7 @@
         n = [None] * len(items)
         terms = []
         for s in range(D):
-            for m, ((r, t), (value, h)) in enumerate(zip(items, coupled(zb, qb, 0, s, items))):
+            for m, ((r, t), (value, h)) in enumerate(zip(items, coupled(zb, qb, s, items))):
                 at = tile_at(r)
                 w = bb[loc[s], at, lanes(t)] - h
                 w_ref[s, at, lanes(t)] = w
@@ -450,6 +466,30 @@
                     f_out[at, lanes(t)] = n[m] * inv[s, at, lanes(t)]
         return curve + tree(terms)
 
+    def start_edge(items, carry):
+        for s in range(D):
+            for (r, t), (_, h) in zip(items, coupled(zb, qb, s, items)):
+                at = tile_at(r)
+                w_ref[s, at, lanes(t)] = bb[loc[s], at, lanes(t)] - h
+        return carry
+
+    def end_edge(left_part, right_part, items, curve):
+        n = [None] * len(items)
+        terms = []
+        for s in range(D):
+            for m, (r, t) in enumerate(items):
+                at = tile_at(r)
+                w = w_ref[s, at, lanes(t)]
+                if t in (0, nt - 1):
+                    w = w - col_term(left_part, right_part, s * ni + r // T, t)
+                    w_ref[s, at, lanes(t)] = w
+                terms.append(zb[s, t, tile_at(r + T), :] * w)
+                n[m] = w if s == 0 else w + gain[s - 1, at, lanes(t)] * n[m]
+                num[s, at, lanes(t)] = n[m]
+                if s == D - 1:
+                    f_out[at, lanes(t)] = n[m] * inv[s, at, lanes(t)]
+        return curve + tree(terms)
+
     def down(value):
         return jnp.sum(value, axis=0, keepdims=True)
 
@@ -479,10 +519,12 @@
     greeted(0)
     greet(1)
     gather_group([full(rho_inner), full(curve_inner)])
+    sides_work(start_edge, ends_work(start_edge, 0))
     halo_wait(z_copies, 0)
-    place_rows(zb, qb, 0)
-
-    curve_edge = edge_work(apply_z, zero)
+    mend_rows(w_ref, 0)
+    end_z = functools.partial(end_edge, zcol_in[0, 1], col_out[...] * zcol_in[0, 0])
+
+    curve_edge = sides_work(end_z, ends_work(end_z, zero))
     f_edge = middle(f_out, f_in, regions[1:], 7)
     for n in range(1, len(hops)):
         greeted(n)
@@ -497,8 +539,10 @@
     carry = inner_work(solve_y, carry)
     for copy in f_edge:
         copy.wait_recv()
-    carry = edge_work(solve_y, carry)
-    y_copies = halo_send(yb, qyb, carry[1], carry[2], 1)
+    carry = ends_work(solve_y, carry)
+    y_copies = send_rows(yb, qyb, 1)
+    carry = sides_work(solve_y, carry)
+    y_copies += send_cols(carry[1], carry[2], 1)
 
     sums = group_sum()
 
@@ -513,7 +557,7 @@
     def apply_y(items, acc):
         terms = [[] for _ in acc]
         for s in range(D):
-            for (r, t), (y, h) in zip(items, coupled(yb, qyb, None, s, items)):
+            for (r, t), (y, h) in zip(items, coupled(yb, qyb, s, items)):
                 at = tile_at(r)
                 w = w_ref[s, at, lanes(t)]
                 v = w - h
@@ -525,11 +569,6 @@
                 for n, term in enumerate((res * pre, w * y, pre * image, y * v, z * v)):
                     terms[n].append(term)
         return tuple(a + tree(b) for a, b in zip(acc, terms))
-
-    for s in range(D):
-        for t in range(nt):
-            yb[s, t, rows + T : rows + 2 * T, :] = zero
-            qyb[s, t, 0:T, :] = zero
 
     def whole(i):
         r = i * T
@@ -573,22 +612,14 @@
             }
             remote(total_out, mine, p_recv, peer, out_sem.at[1]).start()
     pltpu.make_async_copy(total_out, mine, p_recv).start()
-    for s in range(D):
-        for t in range(nt):
-            v_ref[s, 0:1, lanes(t)] = v_ref[s, 0:1, lanes(t)] - zrow_in[1, 1, s, t : t + 1, :]
-            v_ref[s, rows - 1 : rows, lanes(t)] = (
-                v_ref[s, rows - 1 : rows, lanes(t)] - row_out[s, t : t + 1, :] * zrow_in[1, 0, s, t : t + 1, :]
-            )
-    right_part = col_out[...] * zcol_in[1, 0]
-    left_part = zcol_in[1, 1]
+    mend_rows(v_ref, 1)
+    left_part, right_part = zcol_in[1, 1], col_out[...] * zcol_in[1, 0]
 
     def mend(i, carry):
         at = tile_at(i * T)
         for s in range(D):
-            k = s * ni + i
-            first, final = lanes(0), lanes(nt - 1)
-            v_ref[s, at, first] = v_ref[s, at, first] - jnp.where(lane == 0, spread(left_part, k, 0), 0.0)
-            v_ref[s, at, final] = v_ref[s, at, final] - jnp.where(lane == W - 1, spread(right_part, k, W - 1), 0.0)
+            for t in (0, nt - 1):
+                v_ref[s, at, lanes(t)] = v_ref[s, at, lanes(t)] - col_term(left_part, right_part, s * ni + i, t)
         return carry
 
     lax.fori_loop(0, ni, mend, 0)

time: 32.7 us -> 31.5 us (0.963)
  Pallas kernels: 31.9 us -> 30.8 us
    pallas_call x1, Pallas kernels: 29.8 us -> 28.6 us  [step(): pl.pallas_call(functools.partial(kernel, (rows, cols), (layers, pxs, pys)...]
where the time goes in v6:
time: 31.5 us; the launch traced here: 31.4 us
  Pallas kernels  30.8 us (98%)
  between operations  0.64 us (2%)
    pallas_call x1, Pallas kernels, step(): pl.pallas_call(functools.partial(kernel, (rows, cols), (layers, pxs, pys)...  28.6 us
    pallas_call x1, Pallas kernels, step(): pl.pallas_call(functools.partial(finish, (rows, cols)), out_shape=(out(*b...  2.16 us

profile of v6, /device:TPU:1, one launch (start us, length us, event | category | flops | bytes accessed | tf_op | source)
XLA Modules:
  0.0 31.4 jit_solution(4273816027930837682)
XLA Ops:
  0.6 28.6 %shard_map.77 = (f32[4,128,1024]{2,1,0:T(8,128)S(1)}, f32[4,8,144,128]{3,2,1,0:T(8,128)S(1)}, f32[4,8,144,128]{3,2,1,0:T(8,128)S(1)}, f32[4,128,1024]{2,1,0:T(8,...) custom-call(f32[4,128,1024]{2,1,0:T(8,128)} %refs_0_.1, f32[4,128,1024]{2,1,0:T(8,128)} %refs_1_.1, ...), custom_call_target="tpu_custom_call" | custom-call | tf_op jit(solution)/shard_map/pallas_call | solution.py:714
  29.2 2.2 %shard_map.78 = (f32[4,128,1024]{2,1,0:T(8,128)}, f32[4,128,1024]{2,1,0:T(8,128)}) custom-call(f32[4,128,1024]{2,1,0:T(8,128)S(1)} %get-tuple-element.8.bb, f32[4,8,144,128]{3,2,1,0:T(8,128)S(1)} %get-tuple-element.9.zb, f32[4,8,144,128]{3,2,1,0:T(8,128)S(1)} %get-tuple-element.10.yb, f32[4,128,1024]{2,1,0:T(8,128)S(1)} %get-tuple-element.11.w_ref, ...), custom_call_target="tpu_custom_call" | custom-call | tf_op jit(solution)/shard_map/pallas_call | solution.py:724

commit v7 on v6

--- a/solution.py
+++ b/solution.py
@@ -16,7 +16,7 @@
 
 def kernel(shape, counts, *refs):
     dma = pltpu.SemaphoreType.DMA
-    pl.run_scoped(functools.partial(solve_all, shape, counts, *refs), dma((28,)), dma((32,)))
+    pl.run_scoped(functools.partial(solve_all, shape, counts, *refs), dma((34,)), dma((34,)))
 
 
 def solve_all(
@@ -82,20 +82,26 @@
         for copy in top_loads:
             copy.start()
 
-    chunks = 4
-    step = rows // chunks
+    quarter = rows // 4
+    stops = [0, quarter, 2 * quarter, 3 * quarter]
+    if quarter >= 4 * T:
+        stops.append(rows - 2 * T)
+    stops.append(rows)
+    chunks = list(zip(stops, stops[1:]))
     chunk_loads = []
-    for c in range(chunks):
-        at = pl.ds(c * step, step)
-        short = step - T if c == chunks - 1 else step
-        chunk_loads.append([
-            load(rw_hbm.at[:, pl.ds(c * step, short), :], rwp.at[:, pl.ds(T + c * step, short), :]),
+    for lo, hi in chunks:
+        at = pl.ds(lo, hi - lo)
+        short = pl.ds(lo, min(hi, rows - T) - lo)
+        chunk_loads.append([] if lo >= rows - T else [
+            load(rw_hbm.at[:, short, :], rwp.at[:, pl.ds(T + lo, min(hi, rows - T) - lo), :]),
+        ])
+        chunk_loads[-1] += [
             load(cl_hbm.at[:, at, 0:last], cl.at[:, at, 0:last]),
             load(vi_hbm.at[0 : D - 1, at, :], vi.at[0 : D - 1, at, :]),
             load(mk_hbm.at[0 : D - 1, at, :], mk.at[0 : D - 1, at, :]),
             load(gd_hbm.at[:, at, :], gd.at[:, at, :]),
             load(b_hbm.at[:, at, :], bb.at[:, at, :]),
-        ])
+        ]
         for copy in chunk_loads[-1]:
             copy.start()
 
@@ -151,11 +157,9 @@
     gate(has_lower, row_copy.start)
     for peer in near:
         pl.semaphore_signal(far_sem.at[0], inc=1, device_id=peer, device_id_type=MESH)
-    pieces = chunks
-    piece = rows // pieces
     c3_copies = [
-        remote(c3.at[pl.ds(c * piece, piece)], c3.at[pl.ds(c * piece, piece)], s_recv.at[2 + c], partner)
-        for c in range(pieces)
+        remote(c3.at[pl.ds(lo, hi - lo)], c3.at[pl.ds(lo, hi - lo)], s_recv.at[2 + c], partner)
+        for c, (lo, hi) in enumerate(chunks)
     ]
 
     def join(i, carry):
@@ -167,9 +171,9 @@
     def _():
         for copy in top_loads:
             copy.wait()
-        for c in range(pieces):
-            lax.fori_loop(c * piece // T, (c + 1) * piece // T, join, 0)
-            c3_copies[c].start()
+        for (lo, hi), copy in zip(chunks, c3_copies):
+            lax.fori_loop(lo // T, hi // T, join, 0)
+            copy.start()
 
     gated = [(has_lower, row_copy), (has_right, col_copy)]
     sends = []
@@ -257,8 +261,10 @@
                     fg_out[1, at, lanes(t)] = g[m]
         return carry
 
+    cut = max(2, 9 * ni // 16)
     regions = [
-        (pl.ds(T, rows - 2 * T), pl.ds(W, cols - 2 * W)),
+        (pl.ds(T, (cut - 1) * T), pl.ds(W, cols - 2 * W)),
+        (pl.ds(cut * T, (ni - 1 - cut) * T), pl.ds(W, cols - 2 * W)),
         (pl.ds(0, rows), pl.ds(0, W)),
         (pl.ds(0, rows), pl.ds(cols - W, W)),
         (pl.ds(0, T), pl.ds(W, cols - 2 * W)),
@@ -283,16 +289,14 @@
         return [(r, t) for t in range(1, nt)]
 
     fg_inner = []
-    for c in range(chunks):
+    for c, (lo, hi) in enumerate(chunks):
         for copy in chunk_loads[c]:
             copy.wait()
         gate(jnp.logical_not(bottom), c3_copies[c].wait_recv)
-        lo, hi = max(T, c * step), (c + 1) * step
+        lo = max(T, lo)
         lax.fori_loop(lo // T, hi // T, lambda i, x: factor(deep(i), x), 0)
         fg_inner += middle(fg_out, fg_in, [(pl.ds(lo, hi - lo), pl.ds(W, cols - W))], c)
 
-    pl.semaphore_wait(far_sem.at[0], len(near))
-    greet(0)
     gate(has_left, col_copy.wait_recv)
     gate(has_upper, row_copy.wait_recv)
     for s in range(D):
@@ -305,7 +309,9 @@
         lambda j, x: factor([(j * group_of * T + m * T, 0) for m in range(group_of)], x), 0,
     )
     lax.fori_loop(0, 1, lambda i, x: factor(deep(i), x), 0)
-    fg_edge = middle(fg_out, fg_in, [(pl.ds(0, rows), pl.ds(0, W)), (pl.ds(0, T), pl.ds(W, cols - W))], 4)
+    pl.semaphore_wait(far_sem.at[0], len(near))
+    greet(0)
+    fg_edge = middle(fg_out, fg_in, [(pl.ds(0, rows), pl.ds(0, W)), (pl.ds(0, T), pl.ds(W, cols - W))], len(chunks))
 
     def solve(first, z, q, f_ref, items, carry):
         rho, pack_l, pack_r = carry
@@ -410,7 +416,8 @@
     solve_z = functools.partial(solve, True, zb, qb, None)
     for copy in fg_inner:
         copy.wait_recv()
-    rho_inner = inner_work(solve_z, (zero, zero, zero))[0]
+    rho_inner = inner_work(solve_z, (zero, zero, zero), 1, cut)[0]
+    rho_rest = inner_work(solve_z, (zero, zero, zero), cut)[0]
     for copy in fg_edge:
         copy.wait_recv()
     carry = ends_work(solve_z, (zero, zero, zero))
@@ -514,8 +521,8 @@
         wait_rows(size1 - 1, g_recv)
         return tree([group[m] for m in range(size1)])
 
-    curve_inner = inner_work(apply_z, zero)
-    f_inner = middle(f_out, f_in, regions[:1], 6)
+    curve_inner = inner_work(apply_z, zero, 1, cut)
+    f_inner = middle(f_out, f_in, regions[:1], len(chunks) + 2)
     greeted(0)
     greet(1)
     gather_group([full(rho_inner), full(curve_inner)])
@@ -525,7 +532,9 @@
     end_z = functools.partial(end_edge, zcol_in[0, 1], col_out[...] * zcol_in[0, 0])
 
     curve_edge = sides_work(end_z, ends_work(end_z, zero))
-    f_edge = middle(f_out, f_in, regions[1:], 7)
+    f_edge = middle(f_out, f_in, regions[2:], len(chunks) + 4)
+    curve_rest = inner_work(apply_z, zero, cut)
+    f_rest = middle(f_out, f_in, regions[1:2], len(chunks) + 3)
     for n in range(1, len(hops)):
         greeted(n)
         greet(n + 1)
@@ -536,13 +545,16 @@
     carry = (zero, zero, zero)
     for copy in f_inner:
         copy.wait_recv()
-    carry = inner_work(solve_y, carry)
+    inner_work(solve_y, carry, 1, cut)
     for copy in f_edge:
         copy.wait_recv()
     carry = ends_work(solve_y, carry)
     y_copies = send_rows(yb, qyb, 1)
     carry = sides_work(solve_y, carry)
     y_copies += send_cols(carry[1], carry[2], 1)
+    for copy in f_rest:
+        copy.wait_recv()
+    inner_work(solve_y, carry, cut)
 
     sums = group_sum()
 
@@ -587,7 +599,7 @@
     acc = (acc[0], acc[1], acc[2] + centre * (edge_z - centre * edge_y), acc[3] - edge_y, acc[4] - edge_z)
 
     s0, s2, t0, t2, zv, rho_own, curve_own = (
-        full(value) for value in acc + (rho_inner + rho_edge, curve_inner + curve_edge)
+        full(value) for value in acc + (rho_inner + rho_rest + rho_edge, curve_inner + curve_rest + curve_edge)
     )
     total_out[...] = line([
         s0, 2.0 * (curve_own - centre * s2), s2,
@@ -706,7 +718,7 @@
             vmem(depth, nt, W), vmem(depth, nt, W), vmem(T, W), vmem(T, W),
             vmem(2, 2, depth, nt, W), vmem(2, 2, depth, nt, W), vmem(2, 2, T, W), vmem(2, 2, T, W),
             vmem(1, 1, W), vmem(size1, 1, W), vmem(1, W), vmem(size1 * pxs, W), vmem(size1 * pxs, 1, W),
-            dma((6,)), dma((8,)), dma((11,)), dma, dma, pltpu.SemaphoreType.REGULAR((4,)), pltpu.SemaphoreType.REGULAR,
+            dma((7,)), dma((8,)), dma((13,)), dma, dma, pltpu.SemaphoreType.REGULAR((4,)), pltpu.SemaphoreType.REGULAR,
         ]
         out = lambda *dims: jax.ShapeDtypeStruct(dims, F32)
         in_vmem = pl.BlockSpec(memory_space=pltpu.VMEM)

time: 31.5 us -> 31.8 us (level)
  no operation moved by 1% of the time
where the time goes in v7:
time: 31.8 us; the launch traced here: 31.7 us
  Pallas kernels  31 us (97%)
  between operations  0.64 us (2%)
    pallas_call x1, Pallas kernels, step(): pl.pallas_call(functools.partial(kernel, (rows, cols), (layers, pxs, pys)...  28.9 us
    pallas_call x1, Pallas kernels, step(): pl.pallas_call(functools.partial(finish, (rows, cols)), out_shape=(out(*b...  2.16 us

profile of v7, /device:TPU:1, one launch (start us, length us, event | category | flops | bytes accessed | tf_op | source)
XLA Modules:
  0.0 31.7 jit_solution(4858295467535657519)
XLA Ops:
  0.6 28.9 %shard_map.77 = (f32[4,128,1024]{2,1,0:T(8,128)S(1)}, f32[4,8,144,128]{3,2,1,0:T(8,128)S(1)}, f32[4,8,144,128]{3,2,1,0:T(8,128)S(1)}, f32[4,128,1024]{2,1,0:T(8,...) custom-call(f32[4,128,1024]{2,1,0:T(8,128)} %refs_0_.1, f32[4,128,1024]{2,1,0:T(8,128)} %refs_1_.1, ...), custom_call_target="tpu_custom_call" | custom-call | tf_op jit(solution)/shard_map/pallas_call | solution.py:726
  29.5 2.2 %shard_map.78 = (f32[4,128,1024]{2,1,0:T(8,128)}, f32[4,128,1024]{2,1,0:T(8,128)}) custom-call(f32[4,128,1024]{2,1,0:T(8,128)S(1)} %get-tuple-element.8.bb, f32[4,8,144,128]{3,2,1,0:T(8,128)S(1)} %get-tuple-element.9.zb, f32[4,8,144,128]{3,2,1,0:T(8,128)S(1)} %get-tuple-element.10.yb, f32[4,128,1024]{2,1,0:T(8,128)S(1)} %get-tuple-element.11.w_ref, ...), custom_call_target="tpu_custom_call" | custom-call | tf_op jit(solution)/shard_map/pallas_call | solution.py:736

commit v8 on v7

--- a/solution.py
+++ b/solution.py
@@ -74,8 +74,8 @@
     cl_edge = load(cl_hbm.at[:, :, last : last + W], cl.at[:, :, last : last + W])
     rw_edge = load(rw_hbm.at[:, rows - T : rows, :], rwp.at[:, rows : rows + T, :])
     top_loads = [load(vi_hbm.at[D - 1], vi.at[D - 1]), load(mk_hbm.at[D - 1], mk.at[D - 1])]
+    rw_edge.start()
     cl_edge.start()
-    rw_edge.start()
 
     @pl.when(bottom)
     def _():
@@ -153,8 +153,8 @@
     pl.semaphore_wait(barrier, len(near))
     row_copy = remote(row_out, row_in, s_recv.at[0], px_peer(1))
     col_copy = remote(col_out, col_in, s_recv.at[1], py_peer(1))
+    gate(has_lower, row_copy.start)
     gate(has_right, col_copy.start)
-    gate(has_lower, row_copy.start)
     for peer in near:
         pl.semaphore_signal(far_sem.at[0], inc=1, device_id=peer, device_id_type=MESH)
     c3_copies = [
@@ -523,8 +523,6 @@
 
     curve_inner = inner_work(apply_z, zero, 1, cut)
     f_inner = middle(f_out, f_in, regions[:1], len(chunks) + 2)
-    greeted(0)
-    greet(1)
     gather_group([full(rho_inner), full(curve_inner)])
     sides_work(start_edge, ends_work(start_edge, 0))
     halo_wait(z_copies, 0)
@@ -535,12 +533,8 @@
     f_edge = middle(f_out, f_in, regions[2:], len(chunks) + 4)
     curve_rest = inner_work(apply_z, zero, cut)
     f_rest = middle(f_out, f_in, regions[1:2], len(chunks) + 3)
-    for n in range(1, len(hops)):
-        greeted(n)
-        greet(n + 1)
-    for d in range(1, size1):
-        pl.semaphore_signal(met_sem, inc=1, device_id=group_peer(d), device_id_type=MESH)
-
+    greeted(0)
+    greet(1)
     solve_y = functools.partial(solve, False, yb, qyb, f_in)
     carry = (zero, zero, zero)
     for copy in f_inner:
@@ -556,6 +550,11 @@
         copy.wait_recv()
     inner_work(solve_y, carry, cut)
 
+    for n in range(1, len(hops)):
+        greeted(n)
+        greet(n + 1)
+    for d in range(1, size1):
+        pl.semaphore_signal(met_sem, inc=1, device_id=group_peer(d), device_id_type=MESH)
     sums = group_sum()
 
     def pick(value, n):

time: 31.8 us -> 31.8 us (level)
  no operation moved by 1% of the time
where the time goes in v8:
time: 31.8 us; the launch traced here: 31.7 us
  Pallas kernels  31.1 us (98%)
  between operations  0.64 us (2%)
    pallas_call x1, Pallas kernels, step(): pl.pallas_call(functools.partial(kernel, (rows, cols), (layers, pxs, pys)...  28.9 us
    pallas_call x1, Pallas kernels, step(): pl.pallas_call(functools.partial(finish, (rows, cols)), out_shape=(out(*b...  2.16 us

profile of v8, /device:TPU:1, one launch (start us, length us, event | category | flops | bytes accessed | tf_op | source)
XLA Modules:
  0.0 31.7 jit_solution(7976071646290055899)
XLA Ops:
  0.6 28.9 %shard_map.77 = (f32[4,128,1024]{2,1,0:T(8,128)S(1)}, f32[4,8,144,128]{3,2,1,0:T(8,128)S(1)}, f32[4,8,144,128]{3,2,1,0:T(8,128)S(1)}, f32[4,128,1024]{2,1,0:T(8,...) custom-call(f32[4,128,1024]{2,1,0:T(8,128)} %refs_0_.1, f32[4,128,1024]{2,1,0:T(8,128)} %refs_1_.1, ...), custom_call_target="tpu_custom_call" | custom-call | tf_op jit(solution)/shard_map/pallas_call | solution.py:725
  29.5 2.2 %shard_map.78 = (f32[4,128,1024]{2,1,0:T(8,128)}, f32[4,128,1024]{2,1,0:T(8,128)}) custom-call(f32[4,128,1024]{2,1,0:T(8,128)S(1)} %get-tuple-element.8.bb, f32[4,8,144,128]{3,2,1,0:T(8,128)S(1)} %get-tuple-element.9.zb, f32[4,8,144,128]{3,2,1,0:T(8,128)S(1)} %get-tuple-element.10.yb, f32[4,128,1024]{2,1,0:T(8,128)S(1)} %get-tuple-element.11.w_ref, ...), custom_call_target="tpu_custom_call" | custom-call | tf_op jit(solution)/shard_map/pallas_call | solution.py:735

commit v9 on v8

--- a/solution.py
+++ b/solution.py
@@ -526,6 +526,8 @@
     gather_group([full(rho_inner), full(curve_inner)])
     sides_work(start_edge, ends_work(start_edge, 0))
     halo_wait(z_copies, 0)
+    greeted(0)
+    greet(1)
     mend_rows(w_ref, 0)
     end_z = functools.partial(end_edge, zcol_in[0, 1], col_out[...] * zcol_in[0, 0])
 
@@ -533,8 +535,6 @@
     f_edge = middle(f_out, f_in, regions[2:], len(chunks) + 4)
     curve_rest = inner_work(apply_z, zero, cut)
     f_rest = middle(f_out, f_in, regions[1:2], len(chunks) + 3)
-    greeted(0)
-    greet(1)
     solve_y = functools.partial(solve, False, yb, qyb, f_in)
     carry = (zero, zero, zero)
     for copy in f_inner:

time: 31.8 us -> 31.8 us (level)
  no operation moved by 1% of the time
where the time goes in v9:
time: 31.8 us; the launch traced here: 31.7 us
  Pallas kernels  31 us (97%)
  between operations  0.64 us (2%)
    pallas_call x1, Pallas kernels, step(): pl.pallas_call(functools.partial(kernel, (rows, cols), (layers, pxs, pys)...  28.9 us
    pallas_call x1, Pallas kernels, step(): pl.pallas_call(functools.partial(finish, (rows, cols)), out_shape=(out(*b...  2.16 us

profile of v9, /device:TPU:1, one launch (start us, length us, event | category | flops | bytes accessed | tf_op | source)
XLA Modules:
  0.0 31.7 jit_solution(13977594098279380633)
XLA Ops:
  0.6 28.9 %shard_map.77 = (f32[4,128,1024]{2,1,0:T(8,128)S(1)}, f32[4,8,144,128]{3,2,1,0:T(8,128)S(1)}, f32[4,8,144,128]{3,2,1,0:T(8,128)S(1)}, f32[4,128,1024]{2,1,0:T(8,...) custom-call(f32[4,128,1024]{2,1,0:T(8,128)} %refs_0_.1, f32[4,128,1024]{2,1,0:T(8,128)} %refs_1_.1, ...), custom_call_target="tpu_custom_call" | custom-call | tf_op jit(solution)/shard_map/pallas_call | solution.py:725
  29.5 2.2 %shard_map.78 = (f32[4,128,1024]{2,1,0:T(8,128)}, f32[4,128,1024]{2,1,0:T(8,128)}) custom-call(f32[4,128,1024]{2,1,0:T(8,128)S(1)} %get-tuple-element.8.bb, f32[4,8,144,128]{3,2,1,0:T(8,128)S(1)} %get-tuple-element.9.zb, f32[4,8,144,128]{3,2,1,0:T(8,128)S(1)} %get-tuple-element.10.yb, f32[4,128,1024]{2,1,0:T(8,128)S(1)} %get-tuple-element.11.w_ref, ...), custom_call_target="tpu_custom_call" | custom-call | tf_op jit(solution)/shard_map/pallas_call | solution.py:735

commit v10 on v9

--- a/solution.py
+++ b/solution.py
@@ -261,7 +261,7 @@
                     fg_out[1, at, lanes(t)] = g[m]
         return carry
 
-    cut = max(2, 9 * ni // 16)
+    cut = max(2, 12 * ni // 16)
     regions = [
         (pl.ds(T, (cut - 1) * T), pl.ds(W, cols - 2 * W)),
         (pl.ds(cut * T, (ni - 1 - cut) * T), pl.ds(W, cols - 2 * W)),

time: 31.8 us -> 31.4 us (0.987)
  Pallas kernels: 31 us -> 30.6 us
    pallas_call x1, Pallas kernels: 28.9 us -> 28.5 us  [step(): pl.pallas_call(functools.partial(kernel, (rows, cols), (layers, pxs, pys)...]
where the time goes in v10:
time: 31.4 us; the launch traced here: 31.3 us
  Pallas kernels  30.6 us (97%)
  between operations  0.64 us (2%)
    pallas_call x1, Pallas kernels, step(): pl.pallas_call(functools.partial(kernel, (rows, cols), (layers, pxs, pys)...  28.5 us
    pallas_call x1, Pallas kernels, step(): pl.pallas_call(functools.partial(finish, (rows, cols)), out_shape=(out(*b...  2.16 us

profile of v10, /device:TPU:1, one launch (start us, length us, event | category | flops | bytes accessed | tf_op | source)
XLA Modules:
  0.0 31.3 jit_solution(13272586111793076537)
XLA Ops:
  0.6 28.5 %shard_map.77 = (f32[4,128,1024]{2,1,0:T(8,128)S(1)}, f32[4,8,144,128]{3,2,1,0:T(8,128)S(1)}, f32[4,8,144,128]{3,2,1,0:T(8,128)S(1)}, f32[4,128,1024]{2,1,0:T(8,...) custom-call(f32[4,128,1024]{2,1,0:T(8,128)} %refs_0_.1, f32[4,128,1024]{2,1,0:T(8,128)} %refs_1_.1, ...), custom_call_target="tpu_custom_call" | custom-call | tf_op jit(solution)/shard_map/pallas_call | solution.py:725
  29.1 2.2 %shard_map.78 = (f32[4,128,1024]{2,1,0:T(8,128)}, f32[4,128,1024]{2,1,0:T(8,128)}) custom-call(f32[4,128,1024]{2,1,0:T(8,128)S(1)} %get-tuple-element.8.bb, f32[4,8,144,128]{3,2,1,0:T(8,128)S(1)} %get-tuple-element.9.zb, f32[4,8,144,128]{3,2,1,0:T(8,128)S(1)} %get-tuple-element.10.yb, f32[4,128,1024]{2,1,0:T(8,128)S(1)} %get-tuple-element.11.w_ref, ...), custom_call_target="tpu_custom_call" | custom-call | tf_op jit(solution)/shard_map/pallas_call | solution.py:735
